TPU v7x, 512 devices: a 4x2x32 block of a 4x8x32 slice. The times are simulated.
512 devices in a mesh: groups: 2 (over y), pts: 32 (over z), cb: 8 (over x, core).
Axes of the slice: x: 4, y: 2, z: 32, core: 2. Of those that a mesh axis runs over, the one named last changes fastest.
The devices are a block of a 4x8x32 slice.
Arguments:
- points: bfloat16 [131072, 768], P(('groups', 'pts')), parts along dimension 0, may hold values from -60 to 60
- code_one: int32 [131072], P(('groups', 'pts')), parts along dimension 0, may hold values from 0 to 2047
- code_two: int32 [131072], P(('groups', 'pts')), parts along dimension 0, may hold values from 0 to 2047
- cent_one: bfloat16 [4096, 768], P(('groups', 'cb')), parts along dimension 0, may hold values from -6 to 6
- cent_two: bfloat16 [4096, 768], P(('groups', 'cb')), parts along dimension 0, may hold values from -6 to 6
Outputs:
- new_one: bfloat16 [4096, 768], P(('groups', 'cb')), parts along dimension 0
- new_two: bfloat16 [4096, 768], P(('groups', 'cb')), parts along dimension 0
- distortion: float32 [4], P('groups'), parts along dimension 0
There are 2 independent parts, one for each index of `groups`. A program takes and returns all parts, laid end to end along the dimension named above; each array names one. Nothing has to cross between parts.
All inputs are finite; a program needn't handle non-finite values.
Results may differ from a plain program's by a relative error of at most 0.0014.
Values may be sent and summed in bfloat16 or wider, within the bound.
A program may use at most 64 MiB of HBM per device.

v0:
```python
import math

import jax
import jax.numpy as jnp
from jax import lax
from jax.sharding import Mesh
from jax.sharding import PartitionSpec as P

CB = ("cb_0", "cb_1")
PTS_CB = ("pts", "cb_0", "cb_1")
GROUPS_CB = ("groups", "cb_0", "cb_1")


def in_blocks(value, dim, count):
    lengths = value.shape
    tiles = value.reshape(*lengths[:dim], count, lengths[dim] // count, *lengths[dim + 1 :])
    return jnp.moveaxis(tiles, dim, 0)


def sum_at_owner(value, axis, dim):
    count = lax.axis_size(axis)
    tiles = lax.all_to_all(in_blocks(value, dim, count), axis, 0, 0, tiled=True)
    return jnp.sum(tiles, axis=0)


def in_one_piece(arrays, axis, dim, along):
    widths = [math.prod(a.shape[along:]) for a in arrays]
    both = jnp.concatenate(
        [a.reshape(*a.shape[:along], w) for a, w in zip(arrays, widths)], axis=along
    )
    filled = sum_at_owner(both, axis, dim)
    tiles = jnp.split(filled, [sum(widths[:k]) for k in range(1, len(widths))], axis=along)
    return tuple(
        (b.reshape(*filled.shape[:along], *a.shape[along:]) for a, b in zip(arrays, tiles))
    )


def in_order(tiles, dim):
    lengths = list(tiles.shape[1:])
    lengths[dim] *= tiles.shape[0]
    return jnp.moveaxis(tiles, 0, dim).reshape(lengths)


def all_blocks(value, axes, sequence):
    tiles = value
    for k in sequence:
        tiles = lax.all_gather(tiles, axes[k])
    done = sequence[::-1]
    back = [done.index(k) for k in range(len(axes))]
    tiles = tiles.transpose(*back, *range(len(axes), tiles.ndim))
    return tiles.reshape(-1, *value.shape)


def gather_axes(value, axes, sequence, dim):
    return in_order(all_blocks(value, axes, sequence), dim)


def sent_to_all(value, axis):
    copies = jnp.broadcast_to(value, (lax.axis_size(axis), *value.shape))
    return lax.all_to_all(copies, axis, split_axis=0, concat_axis=0, tiled=True)


def gathered_copies(value, axis, dim):
    tiles = sent_to_all(value, axis)
    return in_order(tiles, dim)


def of_everyone(value, axis):
    everything = sent_to_all(value, axis)
    return jnp.sum(everything, axis=0)


def in_one(arrays, axis):
    ends = [0]
    for a in arrays:
        ends.append(ends[-1] + a.size)
    so_far = of_everyone(jnp.concatenate([a.ravel() for a in arrays]), axis)
    return tuple((so_far[b:e].reshape(a.shape) for a, b, e in zip(arrays, ends, ends[1:])))


def nearest_local(data, cents):
    sq = jnp.sum(jnp.square(data.astype(jnp.float32)), axis=1)
    csq = jnp.sum(jnp.square(cents.astype(jnp.float32)), axis=1)
    cross = lax.dot_general(
        data, cents, (((1,), (1,)), ((), ())), preferred_element_type=jnp.float32
    )
    dist = sq[:, None] - 2.0 * cross + csq[None, :]
    local_min = jnp.min(dist, axis=1)
    best = lax.pmin(local_min, CB)
    return jnp.sum(best)


def section_update(data, codes, cents):
    rows = cents.shape[0]
    first = lax.axis_index(CB) * rows
    labels = first + lax.broadcasted_iota(jnp.int32, (1, rows), 1)
    onehot = (codes[:, None] == labels).astype(jnp.bfloat16)
    sums = lax.dot_general(
        onehot, data, (((0,), (0,)), ((), ())), preferred_element_type=jnp.float32
    )
    counts = jnp.sum(onehot.astype(jnp.float32), axis=0)
    share_sums, share_counts = in_one_piece((sums, counts), "pts", 0, 1)
    share_rows = share_sums.shape[0]
    old_rows = lax.dynamic_slice_in_dim(cents, lax.axis_index("pts") * share_rows, share_rows, 0)
    return ((share_sums + old_rows.astype(jnp.float32)) / (share_counts + 1.0)[:, None]).astype(
        jnp.bfloat16
    )


def local(points, code_one, code_two, cent_one, cent_two):
    rows = cent_one.shape[0]
    width = points.shape[1]
    npts = lax.axis_size("pts")
    ncb = lax.axis_size(CB)
    first = lax.axis_index(CB) * rows
    first_local = nearest_local(points, cent_one)
    updated_one = section_update(points, code_one, cent_one)
    gathered = gather_axes(updated_one, PTS_CB, (0, 1, 2), 0)
    share_rows = updated_one.shape[0]
    codebook = jnp.swapaxes(gathered.reshape(npts, ncb, share_rows, width), 0, 1).reshape(
        rows * ncb, width
    )
    new_one = lax.dynamic_slice_in_dim(codebook, first, rows, 0)
    looked = jnp.take(codebook, code_one, axis=0)
    residual = (points.astype(jnp.float32) - looked.astype(jnp.float32)).astype(jnp.bfloat16)
    updated_two = section_update(residual, code_two, cent_two)
    new_two = gathered_copies(updated_two, "pts", 0)
    second_local = nearest_local(residual, cent_two)
    first_sum, second_sum = in_one((first_local, second_local), "pts")
    scale = jnp.float32(points.shape[0] * npts * width)
    distortion = jnp.stack([first_sum, second_sum]) / scale
    return (new_one, new_two, distortion)


def solution(mesh):
    finer = Mesh(
        mesh.devices.reshape(mesh.shape["groups"], mesh.shape["pts"], 4, 2),
        ("groups", "pts", "cb_0", "cb_1"),
    )
    return jax.shard_map(
        local,
        mesh=finer,
        in_specs=(
            P(("groups", "pts"), None),
            P(("groups", "pts")),
            P(("groups", "pts")),
            P(GROUPS_CB, None),
            P(GROUPS_CB, None),
        ),
        out_specs=(P(GROUPS_CB, None), P(GROUPS_CB, None), P("groups")),
        check_vma=False,
    )
```

profile of v0, /device:TPU:38, one launch (start us, length us, event | category | flops | bytes accessed | tf_op | source)
XLA Modules:
  0.0 511.8 jit_solution(11749067723759808798)
XLA Ops:
  7.2 2.1 convert_reduce_fusion
  9.3 0.2 concatenate.26
  9.6 3.2 fusion.12
  12.7 0.0 copy-start.3
  12.8 1.0 pad_maximum_fusion
  13.8 45.8 %all-to-all-start = ((f32[32,8,769]{2,1,0:T(8,128)}), f32[32,8,769]{2,1,0:T(8,128)S(1)}, u32[]{:S(2)}, u32[]{:S(2)}) async-start(f32[32,8,769]{2,1,0:T(8,128)} %pad_maximum_fusion), calls=%async_computation | async-start | bytes 1835008 | tf_op jit(solution)/shard_map/all_to_all | solution.py:22
  59.5 0.1 all-gather.6.cloned.1.call-start
  59.6 95.4 %all-to-all-done = f32[32,8,769]{2,1,0:T(8,128)S(1)} async-done(((f32[32,8,769]{2,1,0:T(8,128)}), f32[32,8,769]{2,1,0:T(8,128)S(1)}, u32[]{:S(2)}, u32[]{:S(2)}) %all-to-all-start) | async-done | bytes 787488 | tf_op jit(solution)/shard_map/all_to_all | solution.py:22
  155.0 0.1 reduce_sum.100
  155.1 0.1 fusion.28
  155.2 0.8 fusion.25
  156.0 58.7 %all-gather = bf16[256,768]{1,0:T(8,128)(2,1)} all-gather(bf16[8,768]{1,0:T(8,128)(2,1)S(1)} %fusion.25), channel_id=2, replica_groups=mesh['groups'=2,'pts'=32,'cb_0'=4,'cb_1'=2] {'pts'}, dimensions={0}, use_global_device_ids=true | all-gather | bytes 405504 | tf_op jit(solution)/shard_map/all_gather | solution.py:47
  214.7 0.1 all-gather.6.cloned.1.call-update
  214.7 0.1 all-gather.8.cloned.1.call-start
  214.8 29.5 %all-gather.6.cloned.1.call-done = bf16[128,8,768]{2,1,0:T(8,128)(2,1)} async-done(((bf16[32,8,768]{2,1,0:T(8,128)(2,1)}), bf16[128,8,768]{2,1,0:T(8,128)(2,1)}) %all-gather.6.cloned.1.call-update) | async-done | bytes 1572880 | tf_op jit(solution)/shard_map/all_gather | solution.py:47
  244.3 0.1 all-gather.8.cloned.1.call-update
  244.3 0.2 concatenate.27
  244.5 0.0 copy-done.3
  244.6 34.0 %all-gather.8.cloned.1.call-done = bf16[8,32,8,768]{3,2,1,0:T(8,128)(2,1)} async-done(((bf16[4,32,8,768]{3,2,1,0:T(8,128)(2,1)}), bf16[8,32,8,768]{3,2,1,0:T(8,128)(2,1)}) %all-gather.8.cloned.1.call-update) | async-done | bytes 3145744 | tf_op jit(solution)/shard_map/all_gather | solution.py:47
  278.6 2.3 copy.23
  280.9 0.2 copy.24
  281.1 9.4 %gather_fusion = bf16[2048,768]{1,0:T(8,128)(2,1)} fusion(bf16[2048,768]{1,0:T(8,128)(2,1)S(1)} %bitcast.22, s32[2048]{0:T(1024)S(1)} %fusion.26), kind=kCustom, calls=%fused_computation | custom fusion | bytes 6299648 | tf_op jit(solution)/shard_map/jit(_take)/gather | solution.py:124
  290.5 0.0 copy-start.4
  290.5 4.3 multiply_reduce_fusion
  294.8 0.0 copy-start.1
  294.8 1.7 copy-done.1
  296.5 0.0 copy-done.4
  296.5 1.3 fusion.15
  297.8 1.0 pad_maximum_fusion.1
  298.8 23.5 %all-to-all-start.1 = ((f32[32,8,769]{2,1,0:T(8,128)}), f32[32,8,769]{2,1,0:T(8,128)}, u32[]{:S(2)}, u32[]{:S(2)}) async-start(f32[32,8,769]{2,1,0:T(8,128)} %pad_maximum_fusion.1), calls=%async_computation.1 | async-start | bytes 1835008 | tf_op jit(solution)/shard_map/all_to_all | solution.py:22
  322.3 1.2 multiply_reduce_fusion.2
  323.4 1.2 multiply_reduce_fusion.1
  324.6 0.0 copy-start
  324.6 0.0 copy-start.2
  324.6 3.1 fusion.10
  327.8 0.0 copy-done
  327.8 0.0 copy-done.2
  327.8 1.0 fusion.11
  328.8 22.8 %all-reduce = (f32[2048]{0:T(1024)S(1)}, f32[2048]{0:T(1024)S(1)}) all-reduce(f32[2048]{0:T(1024)S(1)} %fusion.10, f32[2048]{0:T(1024)S(1)} %fusion.11), channel_id=1, replica_groups=mesh['groups'=2,'pts'=32,'cb_0'=4,'cb_1'=2] {'cb_0','cb_1'}, use_global_device_ids=true, to_apply=%region_12.13 | all-reduce | flops 4096 | bytes 32768 | tf_op jit(solution)/shard_map/pmin | solution.py:89
  351.6 0.6 reduce_sum.108
  352.2 0.6 reduce_sum.105
  352.8 1.4 pad_maximum_fusion.2
  354.2 64.0 %all-to-all-done.1 = f32[32,8,769]{2,1,0:T(8,128)} async-done(((f32[32,8,769]{2,1,0:T(8,128)}), f32[32,8,769]{2,1,0:T(8,128)}, u32[]{:S(2)}, u32[]{:S(2)}) %all-to-all-start.1) | async-done | bytes 787488 | tf_op jit(solution)/shard_map/all_to_all | solution.py:22
  418.2 0.6 broadcast_in_dim.30
  418.8 5.9 %all-to-all-start.3 = ((f32[32,1,2]{2,1,0:T(1,128)}), f32[32,1,2]{2,1,0:T(1,128)S(1)}, u32[]{:S(2)}, u32[]{:S(2)}) async-start(f32[32,1,2]{2,1,0:T(1,128)} %broadcast_in_dim.30), calls=%async_computation.3 | async-start | bytes 32768 | tf_op jit(solution)/shard_map/all_to_all | solution.py:60
  424.8 1.2 reduce_sum.102
  426.0 0.1 fusion.27
  426.1 0.8 fusion.23
  426.9 19.5 %all-to-all-done.3 = f32[32,1,2]{2,1,0:T(1,128)S(1)} async-done(((f32[32,1,2]{2,1,0:T(1,128)}), f32[32,1,2]{2,1,0:T(1,128)S(1)}, u32[]{:S(2)}, u32[]{:S(2)}) %all-to-all-start.3) | async-done | bytes 288 | tf_op jit(solution)/shard_map/all_to_all | solution.py:60
  446.4 0.8 broadcast_in_dim.29
  447.2 4.8 all-to-all-start.2
  452.0 0.8 constant_dynamic-slice_fusion
  452.7 0.1 reduce_sum.109
  452.8 0.5 broadcast_multiply_fusion
  453.3 50.9 %all-to-all-done.2 = bf16[32,8,768]{2,1,0:T(8,128)(2,1)S(1)} async-done(((bf16[32,8,768]{2,1,0:T(8,128)(2,1)}), bf16[32,8,768]{2,1,0:T(8,128)(2,1)S(1)}, u32[]{:S(2)}, u32[]{:S(2)}) %all-to-all-start.2) | async-done | bytes 393248 | tf_op jit(solution)/shard_map/all_to_all | solution.py:60
  504.2 0.7 copy.29
  (3 shorter events, 0.0 us)
Async XLA Ops:
  12.7 231.8 %copy-start.3 = (s32[2048]{0:T(1024)S(1)}, s32[2048]{0:T(1024)}, u32[]{:S(2)}) copy-start(s32[2048]{0:T(1024)} %param.6) | copy-start | bytes 24580
  13.8 141.3 %all-to-all-start = ((f32[32,8,769]{2,1,0:T(8,128)}), f32[32,8,769]{2,1,0:T(8,128)S(1)}, u32[]{:S(2)}, u32[]{:S(2)}) async-start(f32[32,8,769]{2,1,0:T(8,128)} %pad_maximum_fusion), calls=%async_computation | async-start | bytes 1835008 | tf_op jit(solution)/shard_map/all_to_all | solution.py:22
  59.5 184.7 %all-gather.6.cloned.1.call-start = ((), (), s32[]{:S(2)}) async-start(), calls=%async_computation.4 | async-start | bytes 1966080 | tf_op jit(solution)/shard_map/all_gather | solution.py:47
  214.7 63.9 %all-gather.8.cloned.1.call-start = ((), (), s32[]{:S(2)}) async-start(), calls=%async_computation.5 | async-start | bytes 4718592 | tf_op jit(solution)/shard_map/all_gather | solution.py:47
  290.5 6.0 %copy-start.4 = (s32[2048]{0:T(1024)S(1)}, s32[2048]{0:T(1024)}, u32[]{:S(2)}) copy-start(s32[2048]{0:T(1024)} %param.7) | copy-start | bytes 24580
  294.8 1.7 copy-start.1
  298.8 119.4 %all-to-all-start.1 = ((f32[32,8,769]{2,1,0:T(8,128)}), f32[32,8,769]{2,1,0:T(8,128)}, u32[]{:S(2)}, u32[]{:S(2)}) async-start(f32[32,8,769]{2,1,0:T(8,128)} %pad_maximum_fusion.1), calls=%async_computation.1 | async-start | bytes 1835008 | tf_op jit(solution)/shard_map/all_to_all | solution.py:22
  324.6 3.2 copy-start
  324.6 3.1 copy-start.2
  418.8 27.5 %all-to-all-start.3 = ((f32[32,1,2]{2,1,0:T(1,128)}), f32[32,1,2]{2,1,0:T(1,128)S(1)}, u32[]{:S(2)}, u32[]{:S(2)}) async-start(f32[32,1,2]{2,1,0:T(1,128)} %broadcast_in_dim.30), calls=%async_computation.3 | async-start | bytes 32768 | tf_op jit(solution)/shard_map/all_to_all | solution.py:60
  447.2 57.0 %all-to-all-start.2 = ((bf16[32,8,768]{2,1,0:T(8,128)(2,1)}), bf16[32,8,768]{2,1,0:T(8,128)(2,1)S(1)}, u32[]{:S(2)}, u32[]{:S(2)}) async-start(bf16[32,8,768]{2,1,0:T(8,128)(2,1)} %broadcast_in_dim.29), calls=%async_computation.2 | async-start | bytes 786432 | tf_op jit(solution)/shard_map/all_to_all | solution.py:60
Sparse Core Ops, SparseCore 0:
  214.8 29.3 all-gather.5
  246.4 32.1 all-gather.7
where the time goes:
time: 513 us; the launch traced here: 512 us
  waiting for transfers between devices  293 us (57%)
  blocking collectives  81.5 us (16%)
  starting transfers between devices  80.1 us (16%)
  other arithmetic  17 us (3%)
  local copies, waits for them, and re-layouts  16.9 us (3%)
  between operations  14.3 us (3%)
  matrix products  8.64 us (2%)
    all_to_all x2, waiting for transfers between devices, sum_at_owner(): tiles = lax.all_to_all(in_blocks(value, dim, count), axis, 0, 0, tiled=True)  159 us
    all_to_all x2, waiting for transfers between devices, sent_to_all(): return lax.all_to_all(copies, axis, split_axis=0, concat_axis=0, tiled=True)  70.3 us
    all_to_all x2, starting transfers between devices, sum_at_owner(): tiles = lax.all_to_all(in_blocks(value, dim, count), axis, 0, 0, tiled=True)  69.3 us
    all_gather x2, waiting for transfers between devices, all_blocks(): tiles = lax.all_gather(tiles, axes[k])  63.5 us
    all_gather x1, blocking collectives, all_blocks(): tiles = lax.all_gather(tiles, axes[k])  58.7 us
    pmin x1, blocking collectives, nearest_local(): best = lax.pmin(local_min, CB)  22.8 us
    all_to_all x2, starting transfers between devices, sent_to_all(): return lax.all_to_all(copies, axis, split_axis=0, concat_axis=0, tiled=True)  10.7 us
  transfers between devices with their start and end apart: 6, of which 6 were waited for; matrix products, arithmetic and copies ran while one was open for 2% of the time, Pallas kernels for 0%

commit v1 on v0

v1 whole, which is shorter than its diff:
```python
import functools

import jax
import jax.numpy as jnp
from jax import lax
from jax.experimental import pallas as pl
from jax.experimental.pallas import tpu as pltpu
from jax.sharding import PartitionSpec as P

MESH = pl.DeviceIdType.MESH
F32 = jnp.float32
BF16 = jnp.bfloat16
LANES = 128
HALF = 64
WIN = 4
NEAR = (-2, -1, 1)


def far_first(n):
    order = [n // 2]
    for k in range(n // 2 - 1, 0, -1):
        order += [k, n - k]
    return order


def iota(shape, dim):
    return lax.broadcasted_iota(jnp.int32, shape, dim)


def kernel(nz, nx, pts, code1, code2, cent1, cent2, new1, new2, dist, v, sem):
    z = lax.axis_index("pts")
    cb = lax.axis_index("cb")
    x = cb // 2
    c = cb - 2 * x
    h = x - 2 * (x // 2)
    q = z // WIN
    cl = z - WIN * q
    par = cl - 2 * (cl // 2)
    e = cl // 2
    nq = nz // WIN
    s = 1 - 2 * c
    rows = cent1.shape[0]
    npts = pts.shape[0]
    own = npts // (2 * nx)
    g = 2 * rows // nz
    ch = 3 * g
    FAR = far_first(nq)

    def zed(step):
        return lax.rem(z + step + nz, nz)

    def to_z(t):
        return {"pts": t}

    def to_x(t):
        return {"cb": 2 * t + c}

    sib = {"cb": 2 * x + 1 - c}

    def send(src, dst, ss, rs, where):
        pltpu.make_async_remote_copy(
            src_ref=src, dst_ref=dst, send_sem=ss, recv_sem=rs, device_id=where, device_id_type=MESH
        ).start()

    def wait(ref, sm):
        pltpu.make_async_copy(ref, ref, sm).wait()

    def xed(i):
        return lax.rem(x + i, nx)

    barrier = pltpu.get_barrier_semaphore()
    for step in (-2, -1, 1, 2):
        pl.semaphore_signal(barrier, inc=1, device_id=to_z(zed(step)), device_id_type=MESH)
    for o in range(1, nq):
        pl.semaphore_signal(barrier, inc=1, device_id=to_z(zed(WIN * o)), device_id_type=MESH)
    for i in range(1, nx):
        pl.semaphore_signal(barrier, inc=1, device_id=to_x(xed(i)), device_id_type=MESH)
    pl.semaphore_signal(barrier, inc=1, device_id=sib, device_id_type=MESH)

    tile_a = x + (x + 1) // 2
    tile_b = 1 + 3 * (x // 2)
    col_a = pl.ds(pl.multiple_of(tile_a * LANES, LANES), LANES)
    col_b = pl.ds(pl.multiple_of(tile_b * LANES, LANES), LANES)
    loads = [
        pltpu.make_async_copy(pts.at[:, col_a], v["P"].at[:, 0:LANES], sem["ld"].at[0]),
        pltpu.make_async_copy(pts.at[:, col_b], v["P"].at[:, LANES : 2 * LANES], sem["ld"].at[1]),
        pltpu.make_async_copy(cent1, v["C1"].at[cb], sem["ld"].at[2]),
        pltpu.make_async_copy(cent2, v["C2"].at[cb], sem["ld"].at[3]),
        pltpu.make_async_copy(pts.at[pl.ds(pl.multiple_of(cb * own, own), own), :], v["R1"], sem["ld"].at[4]),
    ]
    for ld in loads:
        ld.start()
    loads[0].wait()
    loads[1].wait()

    blk = 256
    hm_b = iota((blk, LANES), 1) // HALF == h
    hm_g = iota((g, LANES), 1) // HALF == h

    @pl.loop(0, npts // blk)
    def _(i):
        sl = pl.ds(pl.multiple_of(i * blk, blk), blk)
        v["W"][sl, 0:LANES] = v["P"][sl, 0:LANES]
        b = v["P"][sl, LANES : 2 * LANES].astype(F32)
        v["W"][sl, LANES : 2 * LANES] = jnp.where(hm_b, b, 1.0).astype(BF16)

    m16 = (iota((nq, g, LANES), 2) & (g - 1)) == iota((nq, g, LANES), 1)

    def class_of(i):
        t = zed(s * (i - 2 + (i // 2) * (5 - 2 * i)))
        return t, t // WIN, lax.rem(t, WIN)

    def class_sums(i, code, w, S, Sc):
        _, _, ct = class_of(i)
        pt = lax.rem(ct, 2)
        et = ct // 2
        n = 2 * nq * g
        r = iota((n, 1), 0)
        hl = r // (nq * g)
        rq = (r // g) & (nq - 1)
        lab = rows * (2 * (2 * pt + hl) + c) + g * (2 * rq + et) + (r & (g - 1))
        oh = jnp.where(lab == code[...], 1.0, 0.0).astype(BF16)
        out = jnp.dot(oh, w[...], preferred_element_type=F32)
        lo, hi = out[: nq * g], out[nq * g :]
        S[ct, :, 0:g, :] = lo[:, :LANES].reshape(nq, g, LANES)
        S[ct, :, g : 2 * g, :] = hi[:, :LANES].reshape(nq, g, LANES)
        lb = lo[:, LANES:]
        hb = pltpu.roll(hi[:, LANES:], HALF, 1)
        hm = iota(lb.shape, 1) // HALF == h
        S[ct, :, 2 * g :, :] = jnp.where(hm, lb, hb).reshape(nq, g, LANES)
        cnt = jnp.where(hm, hb, lb).reshape(nq, g, LANES)
        Sc[ct] = jnp.sum(jnp.where(m16, cnt, 0.0), axis=1, keepdims=True)

    def class_sends(i, S, Sc, X1, X1c, k):
        t, qt, ct = class_of(i)
        for o in FAR + [0]:
            qd = lax.rem(qt + o, nq)
            send(S.at[ct, qd], X1.at[i, qd], sem["s1"].at[k], sem["r1"].at[k, qd], to_z(t))
        send(Sc.at[ct], X1c.at[i], sem["s1c"].at[k], sem["r1c"].at[k], to_z(t))

    def far_sums(S, Sc, X1, X1c, T, Tc, X2, X2c, k):
        wait(X1c, sem["r1c"].at[k])
        Tc[...] = Sc[cl] + X1c[0] + X1c[1] + X1c[2]
        for o in FAR:
            qd = lax.rem(q + o, nq)
            t = zed(WIN * o)
            wait(X1.at[:, 0], sem["r1"].at[k, qd])
            T[qd] = S[cl, qd] + X1[0, qd] + X1[1, qd] + X1[2, qd]
            send(T.at[qd], X2.at[o - 1], sem["s2"].at[k], sem["r2"].at[k], to_z(t))
            send(Tc.at[qd], X2c.at[o - 1], sem["s2c"].at[k], sem["r2c"].at[k], to_z(t))
        wait(X1.at[:, 0], sem["r1"].at[k, q])
        T[q] = S[cl, q] + X1[0, q] + X1[1, q] + X1[2, q]

    def finish(T, Tc, X2, X2c, C, N, k):
        wait(X2c, sem["r2c"].at[k])
        cnt = Tc[q]
        for o in range(nq - 1):
            cnt = cnt + X2c[o]
        wait(X2, sem["r2"].at[k])
        tot = T[q]
        for o in range(nq - 1):
            tot = tot + X2[o]
        full = jnp.broadcast_to(cnt, (g, LANES))
        diag = (iota((g, LANES), 1) & (HALF - 1)) == iota((g, LANES), 0)
        lo_n = jnp.sum(jnp.where(diag & jnp.logical_not(hm_g), full, 0.0), axis=1, keepdims=True) + 1.0
        hi_n = jnp.sum(jnp.where(diag & hm_g, full, 0.0), axis=1, keepdims=True) + 1.0
        sl = pl.ds(pl.multiple_of(g * (z // 2), g), g)
        at_lo = 2 * (2 * par) + c
        at_hi = 2 * (2 * par + 1) + c
        a_lo = C[at_lo, sl, col_a].astype(F32)
        a_hi = C[at_hi, sl, col_a].astype(F32)
        b_lo = C[at_lo, sl, col_b].astype(F32)
        b_hi = pltpu.roll(C[at_hi, sl, col_b].astype(F32), HALF, 1)
        ci = 2 * par + e
        N[c, ci, q, 0:g, :] = ((tot[0:g] + a_lo) / lo_n).astype(BF16)
        N[c, ci, q, g : 2 * g, :] = ((tot[g : 2 * g] + a_hi) / hi_n).astype(BF16)
        N[c, ci, q, 2 * g :, :] = (
            (tot[2 * g :] + jnp.where(hm_g, b_lo, b_hi)) / jnp.where(hm_g, lo_n, hi_n)
        ).astype(BF16)

    def cidx(t):
        ct = lax.rem(t, WIN)
        return 2 * lax.rem(ct, 2) + ct // 2

    def gather(N, k, twin):
        ci = 2 * par + e

        def near_sends(qs):
            for i in range(3):
                send(N.at[c, ci, qs], N.at[c, ci, qs], sem["sl"].at[k], sem["rl"].at[k, i], to_z(zed(s * NEAR[i])))

        for o in FAR:
            send(N.at[c, ci, q], N.at[c, ci, q], sem["sf"].at[k], sem["rf"].at[k, o - 1], to_z(zed(WIN * o)))
        near_sends(q)
        for o in FAR[::-1]:
            qs = lax.rem(q - o + nq, nq)
            wait(N.at[c, ci, qs], sem["rf"].at[k, o - 1])
            near_sends(qs)
        if twin:
            send(N.at[c, ci], N.at[c, ci], sem["st"].at[0], sem["rt"].at[0], sib)
        for i in (2, 1, 0):
            cs = cidx(zed(-s * NEAR[i]))
            wait(N.at[c, cs], sem["rl"].at[k, i])
            if twin:
                send(N.at[c, cs], N.at[c, cs], sem["st"].at[0], sem["rt"].at[0], sib)

    def out_parts(N, t):
        pair = pl.ds(2 * (t // 2), 2)
        rs = pl.ds(pl.multiple_of(g * lax.rem(t, 2), g), g)
        return N.at[c, pair, :, rs, :], N.at[c, pair, :, pl.ds(2 * g, g), :]

    def out_sends(N, OA, OB, k):
        for i in range(1, nx):
            t = xed(i)
            a, b = out_parts(N, t)
            send(a, OA.at[x], sem["so"].at[k, 0], sem["ro"].at[k, 0], to_x(t))
            send(b, OB.at[x], sem["so"].at[k, 1], sem["ro"].at[k, 1], to_x(t))
        a, b = out_parts(N, x)
        pltpu.make_async_copy(a, OA.at[x], sem["lo"].at[k, 0]).start()
        pltpu.make_async_copy(b, OB.at[x], sem["lo"].at[k, 1]).start()

    left = iota((g, LANES), 1) < HALF

    def out_rows(OA, OB, out, k):
        wait(OA.at[0], sem["lo"].at[k, 0])
        wait(OB.at[0], sem["lo"].at[k, 1])
        wait(OA.at[pl.ds(0, nx - 1)], sem["ro"].at[k, 0])
        wait(OB.at[pl.ds(0, nx - 1)], sem["ro"].at[k, 1])
        for ee in range(2):
            for qq in range(nq):
                r0 = g * (2 * qq + ee)
                for xx in range(nx):
                    ta = xx + (xx + 1) // 2
                    out[r0 : r0 + g, ta * LANES : (ta + 1) * LANES] = OA[xx, ee, qq]
                for y in range(nx // 2):
                    two = []
                    for xx in (2 * y, 2 * y + 1):
                        b = OB[xx, ee, qq].astype(F32)
                        two.append(jnp.where(h == 1, pltpu.roll(b, HALF, 1), b))
                    tb = 1 + 3 * y
                    out[r0 : r0 + g, tb * LANES : (tb + 1) * LANES] = jnp.where(left, two[0], two[1]).astype(BF16)

    def nearest(C, R):
        def body(k, m):
            ck = C[k]
            cross = lax.dot_general(ck, R[...], (((1,), (1,)), ((), ())), preferred_element_type=F32)
            cf = ck.astype(F32)
            csq = jnp.sum(cf * cf, axis=1, keepdims=True)
            d = csq - 2.0 * cross
            return jnp.minimum(m, jnp.min(d.reshape(rows // 8, 8, own), axis=0))

        m = lax.fori_loop(0, 2 * nx, body, jnp.full((8, own), jnp.inf, F32))
        mins = jnp.min(m, axis=0, keepdims=True)
        r = R[...].astype(F32)
        psq = jnp.sum(jnp.sum(r * r, axis=0, keepdims=True), axis=1, keepdims=True)
        return jnp.sum(mins, axis=1, keepdims=True) + psq

    @pl.loop(0, WIN)
    def _(i):
        class_sums(i, code1, v["W"], v["S1"], v["Sc1"])

    loads[2].wait()
    loads[3].wait()
    loads[4].wait()
    pl.semaphore_wait(barrier, 4 + (nq - 1) + (nx - 1) + 1)

    for i in range(3):
        class_sends(i, v["S1"], v["Sc1"], v["X11"], v["X1c1"], 0)
    for k, C in enumerate((v["C1"], v["C2"])):
        for i in range(1, nx):
            send(C.at[cb], C.at[cb], sem["sc"].at[k], sem["rc"].at[k], to_x(xed(i)))
        send(C.at[cb], C.at[cb], sem["sct"].at[k], sem["rct"].at[k], sib)

    for b in range(npts // LANES):
        row = code1[0:1, b * LANES : (b + 1) * LANES].astype(F32)
        v["CT"][b * LANES : (b + 1) * LANES, :] = jnp.transpose(jnp.broadcast_to(row, (LANES, LANES)))

    def twin_cents(C, k):
        wait(C.at[pl.ds(0, nx - 1)], sem["rc"].at[k])
        for i in range(1, nx):
            at = 2 * xed(i) + c
            send(C.at[at], C.at[at], sem["sct"].at[k], sem["rct"].at[k], sib)

    far_sums(v["S1"], v["Sc1"], v["X11"], v["X1c1"], v["T1"], v["Tc1"], v["X21"], v["X2c1"], 0)
    twin_cents(v["C1"], 0)
    finish(v["T1"], v["Tc1"], v["X21"], v["X2c1"], v["C1"], v["N1"], 0)
    gather(v["N1"], 0, True)
    out_sends(v["N1"], v["OA1"], v["OB1"], 0)
    wait(v["N1"].at[0], sem["rt"].at[0])

    kb = nq * g
    for cc in range(2):
        for k in range(WIN):
            base = (cc * WIN + k) * 2 * kb
            n = v["N1"][cc, k]
            v["L"][base : base + kb, 0:LANES] = n[:, 0:g, :].reshape(kb, LANES)
            v["L"][base + kb : base + 2 * kb, 0:LANES] = n[:, g : 2 * g, :].reshape(kb, LANES)
            b = n[:, 2 * g :, :].reshape(kb, LANES)
            v["L"][base : base + kb, LANES : 2 * LANES] = b
            v["L"][base + kb : base + 2 * kb, LANES : 2 * LANES] = pltpu.roll(b.astype(F32), HALF, 1).astype(BF16)

    @pl.loop(0, npts // blk)
    def _(i):
        sl = pl.ds(pl.multiple_of(i * blk, blk), blk)
        codes = v["CT"][sl, :]
        parts = []
        lane = iota((1, LANES), 1)
        for j in range(2 * nx * rows // LANES):
            r = lane + j * LANES
            cc = r // (WIN * 2 * kb)
            k = (r // (2 * kb)) & (WIN - 1)
            hl = (r // kb) & 1
            rq = (r // g) & (nq - 1)
            lab = rows * (2 * (2 * (k // 2) + hl) + cc) + g * (2 * rq + (k & 1)) + (r & (g - 1))
            parts.append(jnp.where(codes == lab.astype(F32), 1.0, 0.0).astype(BF16))
        oh = jnp.concatenate(parts, axis=1)
        looked = jnp.dot(oh, v["L"][...], preferred_element_type=F32)
        res = v["P"][sl, :].astype(F32) - looked
        v["W2"][sl, 0:LANES] = res[:, 0:LANES].astype(BF16)
        v["W2"][sl, LANES : 2 * LANES] = jnp.where(hm_b, res[:, LANES:], 1.0).astype(BF16)

    @pl.loop(0, WIN)
    def _(i):
        class_sums(i, code2, v["W2"], v["S2"], v["Sc2"])

        @pl.when(i < 3)
        def _():
            class_sends(i, v["S2"], v["Sc2"], v["X12"], v["X1c2"], 1)

    for i in range(1, nx):
        t = xed(i)
        sl = pl.ds(pl.multiple_of(own * (2 * t + c), own), own)
        send(v["W2"].at[sl, :], v["RR"].at[x], sem["srr"], sem["rrr"], to_x(t))
    sl = pl.ds(pl.multiple_of(own * cb, own), own)
    mine = pltpu.make_async_copy(v["W2"].at[sl, :], v["RR"].at[x], sem["ld"].at[5])
    mine.start()
    far_sums(v["S2"], v["Sc2"], v["X12"], v["X1c2"], v["T2"], v["Tc2"], v["X22"], v["X2c2"], 1)
    twin_cents(v["C2"], 1)
    out_rows(v["OA1"], v["OB1"], new1, 0)

    wait(v["C1"].at[pl.ds(0, nx)], sem["rct"].at[0])
    near_one = nearest(v["C1"], v["R1"])
    mine.wait()
    wait(v["RR"].at[pl.ds(0, nx - 1)], sem["rrr"])
    for xx in range(nx):
        ta = xx + (xx + 1) // 2
        v["R2"][:, ta * LANES : (ta + 1) * LANES] = v["RR"][xx, :, 0:LANES]
    left_own = iota((own, LANES), 1) < HALF
    for y in range(nx // 2):
        tb = 1 + 3 * y
        v["R2"][:, tb * LANES : (tb + 1) * LANES] = jnp.where(
            left_own,
            v["RR"][2 * y, :, LANES:].astype(F32),
            v["RR"][2 * y + 1, :, LANES:].astype(F32),
        ).astype(BF16)
    wait(v["C2"].at[pl.ds(0, nx)], sem["rct"].at[1])
    near_two = nearest(v["C2"], v["R2"])
    lane = iota((1, LANES), 1)
    v["D0"][c] = jnp.where(lane == 0, near_one, jnp.where(lane == 1, near_two, 0.0))
    send(v["D0"].at[c], v["D0"].at[c], sem["sd"].at[0], sem["rd"].at[0], sib)

    finish(v["T2"], v["Tc2"], v["X22"], v["X2c2"], v["C2"], v["N2"], 1)

    wait(v["D0"].at[0], sem["rd"].at[0])
    v["D1"][x] = v["D0"][0] + v["D0"][1]
    for i in range(1, nx):
        send(v["D1"].at[x], v["D1"].at[x], sem["sd"].at[1], sem["rd"].at[1], to_x(xed(i)))

    gather(v["N2"], 1, False)
    out_sends(v["N2"], v["OA2"], v["OB2"], 1)

    wait(v["D1"].at[pl.ds(0, nx - 1)], sem["rd"].at[1])
    tot = v["D1"][0]
    for i in range(1, nx):
        tot = tot + v["D1"][i]
    v["D2"][cl, q] = tot
    for o in FAR:
        send(v["D2"].at[cl, q], v["D2"].at[cl, q], sem["sd"].at[2], sem["rd"].at[2], to_z(zed(WIN * o)))

    out_rows(v["OA2"], v["OB2"], new2, 1)

    wait(v["D2"].at[0, pl.ds(0, nq - 1)], sem["rd"].at[2])
    for i in range(3):
        send(v["D2"].at[cl], v["D2"].at[cl], sem["sd"].at[3], sem["rd"].at[3], to_z(zed(s * NEAR[i])))
    wait(v["D2"].at[pl.ds(0, 3)], sem["rd"].at[3])
    tot = v["D2"][0, 0]
    for i in range(1, nz):
        tot = tot + v["D2"][i // nq, i % nq]
    dist[...] = tot / jnp.float32(npts * nz * pts.shape[1])

    for k in range(2):
        wait(v["X11"], sem["s1"].at[k])
        wait(v["X1c1"], sem["s1c"].at[k])
        wait(v["X21"], sem["s2"].at[k])
        wait(v["X2c1"], sem["s2c"].at[k])
        wait(v["N1"].at[0, 0, pl.ds(0, nq - 1)], sem["sf"].at[k])
        wait(v["N1"].at[0, pl.ds(0, 3)], sem["sl"].at[k])
        wait(v["OA1"].at[pl.ds(0, nx - 1)], sem["so"].at[k, 0])
        wait(v["OB1"].at[pl.ds(0, nx - 1)], sem["so"].at[k, 1])
        wait(v["C1"].at[pl.ds(0, nx - 1)], sem["sc"].at[k])
        wait(v["C1"].at[pl.ds(0, nx)], sem["sct"].at[k])
    wait(v["N1"].at[0], sem["st"].at[0])
    wait(v["RR"].at[pl.ds(0, nx - 1)], sem["srr"])
    wait(v["D0"].at[0], sem["sd"].at[0])
    wait(v["D1"].at[pl.ds(0, nx - 1)], sem["sd"].at[1])
    wait(v["D2"].at[0, pl.ds(0, nq - 1)], sem["sd"].at[2])
    wait(v["D2"].at[pl.ds(0, 3)], sem["sd"].at[3])


def solution(mesh):
    nz = mesh.shape["pts"]
    nx = mesh.shape["cb"] // 2
    nq = nz // WIN

    def local(points, code_one, code_two, cent_one, cent_two):
        npts, width = points.shape
        rows = cent_one.shape[0]
        own = npts // (2 * nx)
        g = 2 * rows // nz
        ch = 3 * g
        vm = pltpu.VMEM
        v = {
            "P": vm((npts, 2 * LANES), BF16),
            "W": vm((npts, 2 * LANES), BF16),
            "W2": vm((npts, 2 * LANES), BF16),
            "CT": vm((npts, LANES), F32),
            "L": vm((2 * nx * rows, 2 * LANES), BF16),
            "R1": vm((own, width), BF16),
            "R2": vm((own, width), BF16),
            "RR": vm((nx, own, 2 * LANES), BF16),
            "D0": vm((2, 1, LANES), F32),
            "D1": vm((nx, 1, LANES), F32),
            "D2": vm((WIN, nq, 1, LANES), F32),
        }
        for k in ("1", "2"):
            v["C" + k] = vm((2 * nx, rows, width), BF16)
            v["S" + k] = vm((WIN, nq, ch, LANES), F32)
            v["Sc" + k] = vm((WIN, nq, 1, LANES), F32)
            v["X1" + k] = vm((3, nq, ch, LANES), F32)
            v["X1c" + k] = vm((3, nq, 1, LANES), F32)
            v["T" + k] = vm((nq, ch, LANES), F32)
            v["Tc" + k] = vm((nq, 1, LANES), F32)
            v["X2" + k] = vm((nq - 1, ch, LANES), F32)
            v["X2c" + k] = vm((nq - 1, 1, LANES), F32)
            v["N" + k] = vm((2, WIN, nq, ch, LANES), BF16)
            v["OA" + k] = vm((nx, 2, nq, g, LANES), BF16)
            v["OB" + k] = vm((nx, 2, nq, g, LANES), BF16)
        dma = pltpu.SemaphoreType.DMA
        sem = {
            "ld": dma((6,)),
            "s1": dma((2,)), "r1": dma((2, nq)), "s1c": dma((2,)), "r1c": dma((2,)),
            "s2": dma((2,)), "r2": dma((2,)), "s2c": dma((2,)), "r2c": dma((2,)),
            "sf": dma((2,)), "rf": dma((2, nq - 1)), "sl": dma((2,)), "rl": dma((2, 3)),
            "st": dma((1,)), "rt": dma((1,)),
            "so": dma((2, 2)), "ro": dma((2, 2)), "lo": dma((2, 2)),
            "sc": dma((2,)), "rc": dma((2,)), "sct": dma((2,)), "rct": dma((2,)),
            "srr": dma(()), "rrr": dma(()),
            "sd": dma((4,)), "rd": dma((4,)),
        }
        hbm = pl.BlockSpec(memory_space=pl.ANY)
        vmem = pl.BlockSpec(memory_space=pltpu.VMEM)
        new_one, new_two, dist = pl.pallas_call(
            functools.partial(kernel, nz, nx),
            out_shape=(
                jax.ShapeDtypeStruct((rows, width), BF16),
                jax.ShapeDtypeStruct((rows, width), BF16),
                jax.ShapeDtypeStruct((1, LANES), F32),
            ),
            in_specs=[hbm, vmem, vmem, hbm, hbm],
            out_specs=(vmem, vmem, vmem),
            scratch_shapes=[v, sem],
            compiler_params=pltpu.CompilerParams(
                collective_id=0, has_side_effects=True, vmem_limit_bytes=60 * 1024 * 1024
            ),
        )(points, code_one.reshape(1, npts), code_two.reshape(1, npts), cent_one, cent_two)
        return new_one, new_two, dist[0, :2]

    cents = P(("groups", "cb"), None)
    return jax.shard_map(
        local,
        mesh=mesh,
        in_specs=(P(("groups", "pts"), None), P(("groups", "pts")), P(("groups", "pts")), cents, cents),
        out_specs=(cents, cents, P("groups")),
        check_vma=False,
    )
```

time: 513 us -> 182 us (0.35)
  waiting for transfers between devices: 293 us -> 0 us
  Pallas kernels: 0 us -> 175 us
  blocking collectives: 81.5 us -> 0 us
  starting transfers between devices: 80.1 us -> 0 us
  other arithmetic: 17 us -> 0 us
  between operations: 14.3 us -> 0.64 us
  local copies, waits for them, and re-layouts: 16.9 us -> 4.62 us
  matrix products: 8.64 us -> 0 us
    all_to_all x4 -> x0, waiting for transfers between devices: 230 us -> none  [the longest x2 159 us: sum_at_owner(): tiles = lax.all_to_all(in_blocks(value, dim, count), axis, 0, 0, tiled=True)]
    pallas_call x0 -> x1, Pallas kernels: none -> 175 us  [local(): pl.pallas_call(functools.partial(kernel, nz, nx), out_shape=(jax.ShapeDty...]
    all_to_all x4 -> x0, starting transfers between devices: 80 us -> none  [the longest x2 69.3 us: sum_at_owner(): tiles = lax.all_to_all(in_blocks(value, dim, count), axis, 0, 0, tiled=True)]
    all_gather x2 -> x0, waiting for transfers between devices: 63.5 us -> none  [all_blocks(): tiles = lax.all_gather(tiles, axes[k])]
    all_gather x1 -> x0, blocking collectives: 58.7 us -> none  [all_blocks(): tiles = lax.all_gather(tiles, axes[k])]
    pmin x1 -> x0, blocking collectives: 22.8 us -> none  [nearest_local(): best = lax.pmin(local_min, CB)]
    reduce_sum x9 -> x0, other arithmetic: 11.4 us -> none  [the longest x1 4.35 us: nearest_local(): sq = jnp.sum(jnp.square(data.astype(jnp.float32)), axis=1)]
    gather x1 -> x0, local copies, waits for them, and re-layouts: 9.38 us -> none  [local(): looked = jnp.take(codebook, code_one, axis=0)]
  transfers between devices with their start and end apart: 6 -> 0, of which waited for: 6 -> 0; matrix products, arithmetic and copies ran while one was open for 2% -> 0% of each run, Pallas kernels for 0% -> 0%
where the time goes in v1:
time: 182 us; the launch traced here: 180 us
  Pallas kernels  175 us (96%)
  local copies, waits for them, and re-layouts  4.62 us (3%)
    pallas_call x1, Pallas kernels, local(): pl.pallas_call(functools.partial(kernel, nz, nx), out_shape=(jax.ShapeDty...  175 us

profile of v1, /device:TPU:38, one launch (start us, length us, event | category | flops | bytes accessed | tf_op | source)
XLA Modules:
  0.0 180.2 jit_solution(16125072545113753558)
XLA Ops:
  0.6 175.0 %shard_map.76 = (bf16[256,768]{1,0:T(8,128)(2,1)}, bf16[256,768]{1,0:T(8,128)(2,1)}, f32[1,128]{1,0:T(1,128)}) custom-call(bf16[2048,768]{1,0:T(8,128)(2,1)} %pts.1, s32[1,2048]{1,0:T(1,128)} %bitcast.4, s32[1,2048]{1,0:T(1,128)} %bitcast.5, bf16[256,768]{1,0:T(8,128)(2,1)} %cent1.1, bf16[256,768]{1,0:T(8,128)(2,1)} %cent2.1), custom_call_target="tpu_custom_call" | custom-call | tf_op jit(solution)/shard_map/pallas_call | solution.py:462
  175.6 1.1 slice_bitcast_fusion
  176.7 1.8 copy.10
  178.5 1.8 copy.11

commit v2 on v1

--- a/solution.py
+++ b/solution.py
@@ -16,11 +16,7 @@
 NEAR = (-2, -1, 1)
 
 
-def far_first(n):
-    order = [n // 2]
-    for k in range(n // 2 - 1, 0, -1):
-        order += [k, n - k]
-    return order
+TREE = (4, 3, -3, 1, -1, 2, -2)
 
 
 def iota(shape, dim):
@@ -44,7 +40,12 @@
     own = npts // (2 * nx)
     g = 2 * rows // nz
     ch = 3 * g
-    FAR = far_first(nq)
+
+    def qm(d):
+        return lax.rem(q + d * s + 2 * nq, nq)
+
+    def zq(d):
+        return lax.rem(z + WIN * d * s + 2 * nz, nz)
 
     def zed(step):
         return lax.rem(z + step + nz, nz)
@@ -133,33 +134,46 @@
 
     def class_sends(i, S, Sc, X1, X1c, k):
         t, qt, ct = class_of(i)
-        for o in FAR + [0]:
-            qd = lax.rem(qt + o, nq)
+        send(Sc.at[ct], X1c.at[i], sem["s1c"].at[k], sem["r1c"].at[k], to_z(t))
+        for d in TREE + (0,):
+            qd = lax.rem(qt + d * s + 2 * nq, nq)
             send(S.at[ct, qd], X1.at[i, qd], sem["s1"].at[k], sem["r1"].at[k, qd], to_z(t))
-        send(Sc.at[ct], X1c.at[i], sem["s1c"].at[k], sem["r1c"].at[k], to_z(t))
-
-    def far_sums(S, Sc, X1, X1c, T, Tc, X2, X2c, k):
-        wait(X1c, sem["r1c"].at[k])
-        Tc[...] = Sc[cl] + X1c[0] + X1c[1] + X1c[2]
-        for o in FAR:
-            qd = lax.rem(q + o, nq)
-            t = zed(WIN * o)
+
+    def far_sums(S, Sc, X1, X1c, T, Tc, XM, X2, X2c, k):
+        for d in TREE + (0,):
+            qd = qm(d)
             wait(X1.at[:, 0], sem["r1"].at[k, qd])
-            T[qd] = S[cl, qd] + X1[0, qd] + X1[1, qd] + X1[2, qd]
-            send(T.at[qd], X2.at[o - 1], sem["s2"].at[k], sem["r2"].at[k], to_z(t))
-            send(Tc.at[qd], X2c.at[o - 1], sem["s2c"].at[k], sem["r2c"].at[k], to_z(t))
-        wait(X1.at[:, 0], sem["r1"].at[k, q])
-        T[q] = S[cl, q] + X1[0, q] + X1[1, q] + X1[2, q]
-
-    def finish(T, Tc, X2, X2c, C, N, k):
+            t = S[cl, qd] + X1[0, qd] + X1[1, qd] + X1[2, qd]
+            if d == 2:
+                wait(XM.at[0], sem["rm"].at[k, 0])
+                wait(XM.at[1], sem["rm"].at[k, 1])
+                t = t + XM[0] + XM[1]
+            if d == -2:
+                wait(XM.at[2], sem["rm"].at[k, 2])
+                t = t + XM[2]
+            T[qd] = t
+            if d == 4:
+                send(T.at[qd], XM.at[0], sem["s2"].at[k], sem["rm"].at[k, 0], to_z(zq(2)))
+                wait(X1c, sem["r1c"].at[k])
+                Tc[...] = Sc[cl] + X1c[0] + X1c[1] + X1c[2]
+                for o in range(1, nq):
+                    qo = lax.rem(q + o, nq)
+                    send(Tc.at[qo], X2c.at[o - 1], sem["s2c"].at[k], sem["r2c"].at[k], to_z(zed(WIN * o)))
+            elif d == 3:
+                send(T.at[qd], XM.at[1], sem["s2"].at[k], sem["rm"].at[k, 1], to_z(zq(1)))
+            elif d == -3:
+                send(T.at[qd], XM.at[2], sem["s2"].at[k], sem["rm"].at[k, 2], to_z(zq(-1)))
+            elif d != 0:
+                at = (1, -1, 2, -2).index(d)
+                send(T.at[qd], X2.at[at], sem["s2"].at[k], sem["r2"].at[k], to_z(zq(d)))
+
+    def finish(T, Tc, X2, X2c, C, k):
         wait(X2c, sem["r2c"].at[k])
         cnt = Tc[q]
         for o in range(nq - 1):
             cnt = cnt + X2c[o]
         wait(X2, sem["r2"].at[k])
-        tot = T[q]
-        for o in range(nq - 1):
-            tot = tot + X2[o]
+        tot = T[q] + X2[0] + X2[1] + X2[2] + X2[3]
         full = jnp.broadcast_to(cnt, (g, LANES))
         diag = (iota((g, LANES), 1) & (HALF - 1)) == iota((g, LANES), 0)
         lo_n = jnp.sum(jnp.where(diag & jnp.logical_not(hm_g), full, 0.0), axis=1, keepdims=True) + 1.0
@@ -171,61 +185,78 @@
         a_hi = C[at_hi, sl, col_a].astype(F32)
         b_lo = C[at_lo, sl, col_b].astype(F32)
         b_hi = pltpu.roll(C[at_hi, sl, col_b].astype(F32), HALF, 1)
-        ci = 2 * par + e
-        N[c, ci, q, 0:g, :] = ((tot[0:g] + a_lo) / lo_n).astype(BF16)
-        N[c, ci, q, g : 2 * g, :] = ((tot[g : 2 * g] + a_hi) / hi_n).astype(BF16)
-        N[c, ci, q, 2 * g :, :] = (
-            (tot[2 * g :] + jnp.where(hm_g, b_lo, b_hi)) / jnp.where(hm_g, lo_n, hi_n)
-        ).astype(BF16)
+        new_lo = ((tot[0:g] + a_lo) / lo_n).astype(BF16)
+        new_hi = ((tot[g : 2 * g] + a_hi) / hi_n).astype(BF16)
+        new_b = ((tot[2 * g :] + jnp.where(hm_g, b_lo, b_hi)) / jnp.where(hm_g, lo_n, hi_n)).astype(BF16)
+        return new_lo, new_hi, new_b
 
     def cidx(t):
         ct = lax.rem(t, WIN)
         return 2 * lax.rem(ct, 2) + ct // 2
 
-    def gather(N, k, twin):
+    def tree(at, k, near_sends):
+        slots = (1, -1, 2, -2, 3, -3, 4)
+
+        def far_send(ref, d, to):
+            send(ref, ref, sem["sf"].at[k], sem["rf"].at[k, slots.index(d)], to_z(zq(to)))
+
+        for d in (2, -2, 1, -1):
+            far_send(at(q), d, d)
+        near_sends(q)
+        for d in slots:
+            qs = qm(-d)
+            wait(at(qs), sem["rf"].at[k, slots.index(d)])
+            if d == 2:
+                far_send(at(qs), 4, 2)
+                far_send(at(qs), 3, 1)
+            if d == -2:
+                far_send(at(qs), -3, -1)
+            near_sends(qs)
+
+    def gather(N):
         ci = 2 * par + e
 
         def near_sends(qs):
             for i in range(3):
-                send(N.at[c, ci, qs], N.at[c, ci, qs], sem["sl"].at[k], sem["rl"].at[k, i], to_z(zed(s * NEAR[i])))
-
-        for o in FAR:
-            send(N.at[c, ci, q], N.at[c, ci, q], sem["sf"].at[k], sem["rf"].at[k, o - 1], to_z(zed(WIN * o)))
-        near_sends(q)
-        for o in FAR[::-1]:
-            qs = lax.rem(q - o + nq, nq)
-            wait(N.at[c, ci, qs], sem["rf"].at[k, o - 1])
-            near_sends(qs)
-        if twin:
-            send(N.at[c, ci], N.at[c, ci], sem["st"].at[0], sem["rt"].at[0], sib)
+                send(N.at[c, ci, qs], N.at[c, ci, qs], sem["sl"].at[0], sem["rl"].at[0, i], to_z(zed(s * NEAR[i])))
+
+        tree(lambda qs: N.at[c, ci, qs], 0, near_sends)
+        send(N.at[c, ci], N.at[c, ci], sem["st"].at[0], sem["rt"].at[0], sib)
         for i in (2, 1, 0):
             cs = cidx(zed(-s * NEAR[i]))
-            wait(N.at[c, cs], sem["rl"].at[k, i])
-            if twin:
-                send(N.at[c, cs], N.at[c, cs], sem["st"].at[0], sem["rt"].at[0], sib)
+            wait(N.at[c, cs], sem["rl"].at[0, i])
+            send(N.at[c, cs], N.at[c, cs], sem["st"].at[0], sem["rt"].at[0], sib)
+
+    def gather_rows(O):
+        def near_sends(qs):
+            at = O.at[2 * qs + e]
+            for i, step in enumerate((1, -1, 2 * s)):
+                send(at, at, sem["sl"].at[1], sem["rl"].at[1, i], to_z(zed(step)))
+
+        tree(lambda qs: O.at[2 * qs + e], 1, near_sends)
 
     def out_parts(N, t):
         pair = pl.ds(2 * (t // 2), 2)
         rs = pl.ds(pl.multiple_of(g * lax.rem(t, 2), g), g)
         return N.at[c, pair, :, rs, :], N.at[c, pair, :, pl.ds(2 * g, g), :]
 
-    def out_sends(N, OA, OB, k):
+    def out_sends(N, OA, OB):
         for i in range(1, nx):
             t = xed(i)
             a, b = out_parts(N, t)
-            send(a, OA.at[x], sem["so"].at[k, 0], sem["ro"].at[k, 0], to_x(t))
-            send(b, OB.at[x], sem["so"].at[k, 1], sem["ro"].at[k, 1], to_x(t))
+            send(a, OA.at[x], sem["so"].at[0], sem["ro"].at[0], to_x(t))
+            send(b, OB.at[x], sem["so"].at[1], sem["ro"].at[1], to_x(t))
         a, b = out_parts(N, x)
-        pltpu.make_async_copy(a, OA.at[x], sem["lo"].at[k, 0]).start()
-        pltpu.make_async_copy(b, OB.at[x], sem["lo"].at[k, 1]).start()
+        pltpu.make_async_copy(a, OA.at[x], sem["lo"].at[0]).start()
+        pltpu.make_async_copy(b, OB.at[x], sem["lo"].at[1]).start()
 
     left = iota((g, LANES), 1) < HALF
 
-    def out_rows(OA, OB, out, k):
-        wait(OA.at[0], sem["lo"].at[k, 0])
-        wait(OB.at[0], sem["lo"].at[k, 1])
-        wait(OA.at[pl.ds(0, nx - 1)], sem["ro"].at[k, 0])
-        wait(OB.at[pl.ds(0, nx - 1)], sem["ro"].at[k, 1])
+    def out_rows(OA, OB, out):
+        wait(OA.at[0], sem["lo"].at[0])
+        wait(OB.at[0], sem["lo"].at[1])
+        wait(OA.at[pl.ds(0, nx - 1)], sem["ro"].at[0])
+        wait(OB.at[pl.ds(0, nx - 1)], sem["ro"].at[1])
         for ee in range(2):
             for qq in range(nq):
                 r0 = g * (2 * qq + ee)
@@ -281,11 +312,15 @@
             at = 2 * xed(i) + c
             send(C.at[at], C.at[at], sem["sct"].at[k], sem["rct"].at[k], sib)
 
-    far_sums(v["S1"], v["Sc1"], v["X11"], v["X1c1"], v["T1"], v["Tc1"], v["X21"], v["X2c1"], 0)
+    far_sums(v["S1"], v["Sc1"], v["X11"], v["X1c1"], v["T1"], v["Tc1"], v["XM1"], v["X21"], v["X2c1"], 0)
     twin_cents(v["C1"], 0)
-    finish(v["T1"], v["Tc1"], v["X21"], v["X2c1"], v["C1"], v["N1"], 0)
-    gather(v["N1"], 0, True)
-    out_sends(v["N1"], v["OA1"], v["OB1"], 0)
+    new_lo, new_hi, new_b = finish(v["T1"], v["Tc1"], v["X21"], v["X2c1"], v["C1"], 0)
+    v["N1"][c, 2 * par + e, q, 0:g, :] = new_lo
+    v["N1"][c, 2 * par + e, q, g : 2 * g, :] = new_hi
+    v["N1"][c, 2 * par + e, q, 2 * g :, :] = new_b
+    gather(v["N1"])
+    twin_cents(v["C2"], 1)
+    out_sends(v["N1"], v["OA1"], v["OB1"])
     wait(v["N1"].at[0], sem["rt"].at[0])
 
     kb = nq * g
@@ -334,9 +369,10 @@
     sl = pl.ds(pl.multiple_of(own * cb, own), own)
     mine = pltpu.make_async_copy(v["W2"].at[sl, :], v["RR"].at[x], sem["ld"].at[5])
     mine.start()
-    far_sums(v["S2"], v["Sc2"], v["X12"], v["X1c2"], v["T2"], v["Tc2"], v["X22"], v["X2c2"], 1)
-    twin_cents(v["C2"], 1)
-    out_rows(v["OA1"], v["OB1"], new1, 0)
+    far_sums(v["S2"], v["Sc2"], v["X12"], v["X1c2"], v["T2"], v["Tc2"], v["XM2"], v["X22"], v["X2c2"], 1)
+    out_rows(v["OA1"], v["OB1"], v["NW"])
+    put_one = pltpu.make_async_copy(v["NW"], new1, sem["ld"].at[6])
+    put_one.start()
 
     wait(v["C1"].at[pl.ds(0, nx)], sem["rct"].at[0])
     near_one = nearest(v["C1"], v["R1"])
@@ -359,29 +395,68 @@
     v["D0"][c] = jnp.where(lane == 0, near_one, jnp.where(lane == 1, near_two, 0.0))
     send(v["D0"].at[c], v["D0"].at[c], sem["sd"].at[0], sem["rd"].at[0], sib)
 
-    finish(v["T2"], v["Tc2"], v["X22"], v["X2c2"], v["C2"], v["N2"], 1)
-
     wait(v["D0"].at[0], sem["rd"].at[0])
     v["D1"][x] = v["D0"][0] + v["D0"][1]
     for i in range(1, nx):
         send(v["D1"].at[x], v["D1"].at[x], sem["sd"].at[1], sem["rd"].at[1], to_x(xed(i)))
-
-    gather(v["N2"], 1, False)
-    out_sends(v["N2"], v["OA2"], v["OB2"], 1)
-
     wait(v["D1"].at[pl.ds(0, nx - 1)], sem["rd"].at[1])
     tot = v["D1"][0]
     for i in range(1, nx):
         tot = tot + v["D1"][i]
     v["D2"][cl, q] = tot
-    for o in FAR:
+    for o in range(1, nq):
         send(v["D2"].at[cl, q], v["D2"].at[cl, q], sem["sd"].at[2], sem["rd"].at[2], to_z(zed(WIN * o)))
 
-    out_rows(v["OA2"], v["OB2"], new2, 1)
-
-    wait(v["D2"].at[0, pl.ds(0, nq - 1)], sem["rd"].at[2])
-    for i in range(3):
-        send(v["D2"].at[cl], v["D2"].at[cl], sem["sd"].at[3], sem["rd"].at[3], to_z(zed(s * NEAR[i])))
+    new_lo, new_hi, new_b = finish(v["T2"], v["Tc2"], v["X22"], v["X2c2"], v["C2"], 1)
+    v["NC"][0:g, :] = new_lo
+    v["NC"][g : 2 * g, :] = new_b
+    v["NC"][2 * g :, :] = new_hi
+    role = x // 2 == par
+    for hl in range(2):
+        t = 2 * par + hl
+        src = v["NC"].at[pl.ds(g * hl, 2 * g), :]
+
+        @pl.when(t != x)
+        def _():
+            send(src, v["Y"].at[x], sem["sy"], sem["ry"], to_x(t))
+
+        @pl.when(t == x)
+        def _():
+            pltpu.make_async_copy(src, v["Y"].at[x], sem["ly"]).start()
+
+    def pass_dist():
+        wait(v["D2"].at[0, pl.ds(0, nq - 1)], sem["rd"].at[2])
+        for i in range(3):
+            send(v["D2"].at[cl], v["D2"].at[cl], sem["sd"].at[3], sem["rd"].at[3], to_z(zed(s * NEAR[i])))
+
+    @pl.when(role)
+    def _():
+        wait(v["Y"].at[pl.ds(0, nx - 1)], sem["ry"])
+        wait(v["Y"].at[0], sem["ly"])
+        mine = 2 * q + e
+        for y in range(nx // 2):
+            two = []
+            for xx in (2 * y, 2 * y + 1):
+                top = v["Y"][xx, 0:g, :].astype(F32)
+                low = v["Y"][xx, g : 2 * g, :].astype(F32)
+                ta = xx + (xx + 1) // 2
+                v["O"][mine, :, ta * LANES : (ta + 1) * LANES] = jnp.where(h == 1, low, top).astype(BF16)
+                two.append(jnp.where(h == 1, pltpu.roll(top, HALF, 1), low))
+            tb = 1 + 3 * y
+            v["O"][mine, :, tb * LANES : (tb + 1) * LANES] = jnp.where(left, two[0], two[1]).astype(BF16)
+        gather_rows(v["O"])
+        pass_dist()
+        wait(v["O"].at[pl.ds(0, nq)], sem["rl"].at[1, 2])
+
+    @pl.when(jnp.logical_not(role))
+    def _():
+        pass_dist()
+        wait(v["O"].at[pl.ds(0, nq)], sem["rl"].at[1, 0])
+        wait(v["O"].at[pl.ds(0, nq)], sem["rl"].at[1, 1])
+
+    put_two = pltpu.make_async_copy(v["O"], new2, sem["ld"].at[7])
+    put_two.start()
+
     wait(v["D2"].at[pl.ds(0, 3)], sem["rd"].at[3])
     tot = v["D2"][0, 0]
     for i in range(1, nz):
@@ -391,20 +466,33 @@
     for k in range(2):
         wait(v["X11"], sem["s1"].at[k])
         wait(v["X1c1"], sem["s1c"].at[k])
-        wait(v["X21"], sem["s2"].at[k])
+        wait(v["X11"].at[0, pl.ds(0, nq - 1)], sem["s2"].at[k])
         wait(v["X2c1"], sem["s2c"].at[k])
-        wait(v["N1"].at[0, 0, pl.ds(0, nq - 1)], sem["sf"].at[k])
-        wait(v["N1"].at[0, pl.ds(0, 3)], sem["sl"].at[k])
-        wait(v["OA1"].at[pl.ds(0, nx - 1)], sem["so"].at[k, 0])
-        wait(v["OB1"].at[pl.ds(0, nx - 1)], sem["so"].at[k, 1])
         wait(v["C1"].at[pl.ds(0, nx - 1)], sem["sc"].at[k])
         wait(v["C1"].at[pl.ds(0, nx)], sem["sct"].at[k])
+    wait(v["N1"].at[0, 0, pl.ds(0, nq - 1)], sem["sf"].at[0])
+    wait(v["N1"].at[0, pl.ds(0, 3)], sem["sl"].at[0])
+    wait(v["OA1"].at[pl.ds(0, nx - 1)], sem["so"].at[0])
+    wait(v["OB1"].at[pl.ds(0, nx - 1)], sem["so"].at[1])
     wait(v["N1"].at[0], sem["st"].at[0])
     wait(v["RR"].at[pl.ds(0, nx - 1)], sem["srr"])
     wait(v["D0"].at[0], sem["sd"].at[0])
     wait(v["D1"].at[pl.ds(0, nx - 1)], sem["sd"].at[1])
     wait(v["D2"].at[0, pl.ds(0, nq - 1)], sem["sd"].at[2])
     wait(v["D2"].at[pl.ds(0, 3)], sem["sd"].at[3])
+
+    @pl.when(role)
+    def _():
+        wait(v["O"].at[pl.ds(0, nq - 1)], sem["sf"].at[1])
+        wait(v["X11"], sem["sl"].at[1])
+        wait(v["Y"].at[0], sem["sy"])
+
+    @pl.when(jnp.logical_not(role))
+    def _():
+        wait(v["Y"].at[pl.ds(0, 2)], sem["sy"])
+
+    put_one.wait()
+    put_two.wait()
 
 
 def solution(mesh):
@@ -432,6 +520,13 @@
             "D1": vm((nx, 1, LANES), F32),
             "D2": vm((WIN, nq, 1, LANES), F32),
         }
+        v["N1"] = vm((2, WIN, nq, ch, LANES), BF16)
+        v["OA1"] = vm((nx, 2, nq, g, LANES), BF16)
+        v["OB1"] = vm((nx, 2, nq, g, LANES), BF16)
+        v["NW"] = vm((rows, width), BF16)
+        v["NC"] = vm((ch, LANES), BF16)
+        v["Y"] = vm((nx, 2 * g, LANES), BF16)
+        v["O"] = vm((2 * nq, g, width), BF16)
         for k in ("1", "2"):
             v["C" + k] = vm((2 * nx, rows, width), BF16)
             v["S" + k] = vm((WIN, nq, ch, LANES), F32)
@@ -440,19 +535,18 @@
             v["X1c" + k] = vm((3, nq, 1, LANES), F32)
             v["T" + k] = vm((nq, ch, LANES), F32)
             v["Tc" + k] = vm((nq, 1, LANES), F32)
-            v["X2" + k] = vm((nq - 1, ch, LANES), F32)
+            v["XM" + k] = vm((3, ch, LANES), F32)
+            v["X2" + k] = vm((4, ch, LANES), F32)
             v["X2c" + k] = vm((nq - 1, 1, LANES), F32)
-            v["N" + k] = vm((2, WIN, nq, ch, LANES), BF16)
-            v["OA" + k] = vm((nx, 2, nq, g, LANES), BF16)
-            v["OB" + k] = vm((nx, 2, nq, g, LANES), BF16)
         dma = pltpu.SemaphoreType.DMA
         sem = {
-            "ld": dma((6,)),
+            "ld": dma((8,)),
             "s1": dma((2,)), "r1": dma((2, nq)), "s1c": dma((2,)), "r1c": dma((2,)),
-            "s2": dma((2,)), "r2": dma((2,)), "s2c": dma((2,)), "r2c": dma((2,)),
+            "rm": dma((2, 3)), "s2": dma((2,)), "r2": dma((2,)), "s2c": dma((2,)), "r2c": dma((2,)),
             "sf": dma((2,)), "rf": dma((2, nq - 1)), "sl": dma((2,)), "rl": dma((2, 3)),
             "st": dma((1,)), "rt": dma((1,)),
-            "so": dma((2, 2)), "ro": dma((2, 2)), "lo": dma((2, 2)),
+            "so": dma((2,)), "ro": dma((2,)), "lo": dma((2,)),
+            "sy": dma(()), "ry": dma(()), "ly": dma(()),
             "sc": dma((2,)), "rc": dma((2,)), "sct": dma((2,)), "rct": dma((2,)),
             "srr": dma(()), "rrr": dma(()),
             "sd": dma((4,)), "rd": dma((4,)),
@@ -463,17 +557,17 @@
             functools.partial(kernel, nz, nx),
             out_shape=(
                 jax.ShapeDtypeStruct((rows, width), BF16),
-                jax.ShapeDtypeStruct((rows, width), BF16),
+                jax.ShapeDtypeStruct((2 * nq, g, width), BF16),
                 jax.ShapeDtypeStruct((1, LANES), F32),
             ),
             in_specs=[hbm, vmem, vmem, hbm, hbm],
-            out_specs=(vmem, vmem, vmem),
+            out_specs=(hbm, hbm, vmem),
             scratch_shapes=[v, sem],
             compiler_params=pltpu.CompilerParams(
                 collective_id=0, has_side_effects=True, vmem_limit_bytes=60 * 1024 * 1024
             ),
         )(points, code_one.reshape(1, npts), code_two.reshape(1, npts), cent_one, cent_two)
-        return new_one, new_two, dist[0, :2]
+        return new_one, new_two.reshape(rows, width), dist[0, :2]
 
     cents = P(("groups", "cb"), None)
     return jax.shard_map(

time: 182 us -> 162 us (0.89); the launches traced: 180 us -> 162 us
  Pallas kernels: 175 us -> 157 us
    pallas_call x1, Pallas kernels: 175 us -> 157 us  [local(): pl.pallas_call(functools.partial(kernel, nz, nx), out_shape=(jax.ShapeDty...]
where the time goes in v2:
time: 162 us
  Pallas kernels  157 us (97%)
  local copies, waits for them, and re-layouts  4.62 us (3%)
    pallas_call x1, Pallas kernels, local(): pl.pallas_call(functools.partial(kernel, nz, nx), out_shape=(jax.ShapeDty...  157 us
    unnamed x2, local copies, waits for them, and re-layouts  3.53 us

profile of v2, /device:TPU:38, one launch (start us, length us, event | category | flops | bytes accessed | tf_op | source)
XLA Modules:
  0.0 162.2 jit_solution(4873498290565827864)
XLA Ops:
  0.6 156.9 %shard_map.76 = (bf16[256,768]{1,0:T(8,128)(2,1)}, bf16[16,16,768]{2,1,0:T(8,128)(2,1)}, f32[1,128]{1,0:T(1,128)}) custom-call(bf16[2048,768]{1,0:T(8,128)(2,1)} %pts.1, s32[1,2048]{1,0:T(1,128)} %bitcast.6, s32[1,2048]{1,0:T(1,128)} %bitcast.7, bf16[256,768]{1,0:T(8,128)(2,1)} %cent1.1, bf16[256,768]{1,0:T(8,128)(2,1)} %cent2.1), custom_call_target="tpu_custom_call" | custom-call | tf_op jit(solution)/shard_map/pallas_call | solution.py:556
  157.6 1.1 slice_bitcast_fusion
  158.6 1.8 %copy.10 = bf16[256,768]{1,0:T(8,128)(2,1)} copy(bf16[256,768]{1,0:T(8,128)(2,1)} %get-tuple-element.12) | data formatting | bytes 786432
  160.4 1.8 %copy.11 = bf16[256,768]{1,0:T(8,128)(2,1)} copy(bf16[256,768]{1,0:T(8,128)(2,1)} %bitcast.5) | data formatting | bytes 786432

commit v3 on v2

--- a/solution.py
+++ b/solution.py
@@ -37,9 +37,8 @@
     s = 1 - 2 * c
     rows = cent1.shape[0]
     npts = pts.shape[0]
-    own = npts // (2 * nx)
+    chip = npts // nx
     g = 2 * rows // nz
-    ch = 3 * g
 
     def qm(d):
         return lax.rem(q + d * s + 2 * nq, nq)
@@ -85,9 +84,9 @@
     loads = [
         pltpu.make_async_copy(pts.at[:, col_a], v["P"].at[:, 0:LANES], sem["ld"].at[0]),
         pltpu.make_async_copy(pts.at[:, col_b], v["P"].at[:, LANES : 2 * LANES], sem["ld"].at[1]),
-        pltpu.make_async_copy(cent1, v["C1"].at[cb], sem["ld"].at[2]),
-        pltpu.make_async_copy(cent2, v["C2"].at[cb], sem["ld"].at[3]),
-        pltpu.make_async_copy(pts.at[pl.ds(pl.multiple_of(cb * own, own), own), :], v["R1"], sem["ld"].at[4]),
+        pltpu.make_async_copy(cent1, v["C1"].at[x], sem["ld"].at[2]),
+        pltpu.make_async_copy(cent2, v["C2"].at[x], sem["ld"].at[3]),
+        pltpu.make_async_copy(pts.at[pl.ds(pl.multiple_of(x * chip, chip), chip), :], v["R1"], sem["ld"].at[4]),
     ]
     for ld in loads:
         ld.start()
@@ -179,8 +178,8 @@
         lo_n = jnp.sum(jnp.where(diag & jnp.logical_not(hm_g), full, 0.0), axis=1, keepdims=True) + 1.0
         hi_n = jnp.sum(jnp.where(diag & hm_g, full, 0.0), axis=1, keepdims=True) + 1.0
         sl = pl.ds(pl.multiple_of(g * (z // 2), g), g)
-        at_lo = 2 * (2 * par) + c
-        at_hi = 2 * (2 * par + 1) + c
+        at_lo = 2 * par
+        at_hi = 2 * par + 1
         a_lo = C[at_lo, sl, col_a].astype(F32)
         a_hi = C[at_hi, sl, col_a].astype(F32)
         b_lo = C[at_lo, sl, col_b].astype(F32)
@@ -278,13 +277,12 @@
             cf = ck.astype(F32)
             csq = jnp.sum(cf * cf, axis=1, keepdims=True)
             d = csq - 2.0 * cross
-            return jnp.minimum(m, jnp.min(d.reshape(rows // 8, 8, own), axis=0))
-
-        m = lax.fori_loop(0, 2 * nx, body, jnp.full((8, own), jnp.inf, F32))
-        mins = jnp.min(m, axis=0, keepdims=True)
+            return jnp.minimum(m, jnp.min(d.reshape(rows // 8, 8, chip), axis=0))
+
+        m = lax.fori_loop(0, nx, body, jnp.full((8, chip), jnp.inf, F32))
         r = R[...].astype(F32)
         psq = jnp.sum(jnp.sum(r * r, axis=0, keepdims=True), axis=1, keepdims=True)
-        return jnp.sum(mins, axis=1, keepdims=True) + psq
+        return jnp.min(m, axis=0, keepdims=True), psq
 
     @pl.loop(0, WIN)
     def _(i):
@@ -299,27 +297,21 @@
         class_sends(i, v["S1"], v["Sc1"], v["X11"], v["X1c1"], 0)
     for k, C in enumerate((v["C1"], v["C2"])):
         for i in range(1, nx):
-            send(C.at[cb], C.at[cb], sem["sc"].at[k], sem["rc"].at[k], to_x(xed(i)))
-        send(C.at[cb], C.at[cb], sem["sct"].at[k], sem["rct"].at[k], sib)
+            send(C.at[x], C.at[x], sem["sc"].at[k], sem["rc"].at[k], to_x(xed(i)))
 
     for b in range(npts // LANES):
         row = code1[0:1, b * LANES : (b + 1) * LANES].astype(F32)
         v["CT"][b * LANES : (b + 1) * LANES, :] = jnp.transpose(jnp.broadcast_to(row, (LANES, LANES)))
 
-    def twin_cents(C, k):
-        wait(C.at[pl.ds(0, nx - 1)], sem["rc"].at[k])
-        for i in range(1, nx):
-            at = 2 * xed(i) + c
-            send(C.at[at], C.at[at], sem["sct"].at[k], sem["rct"].at[k], sib)
-
     far_sums(v["S1"], v["Sc1"], v["X11"], v["X1c1"], v["T1"], v["Tc1"], v["XM1"], v["X21"], v["X2c1"], 0)
-    twin_cents(v["C1"], 0)
+    wait(v["C1"].at[pl.ds(0, nx - 1)], sem["rc"].at[0])
+    mins_one, psq_one = nearest(v["C1"], v["R1"])
+    v["D0"][c, 0] = mins_one
     new_lo, new_hi, new_b = finish(v["T1"], v["Tc1"], v["X21"], v["X2c1"], v["C1"], 0)
     v["N1"][c, 2 * par + e, q, 0:g, :] = new_lo
     v["N1"][c, 2 * par + e, q, g : 2 * g, :] = new_hi
     v["N1"][c, 2 * par + e, q, 2 * g :, :] = new_b
     gather(v["N1"])
-    twin_cents(v["C2"], 1)
     out_sends(v["N1"], v["OA1"], v["OB1"])
     wait(v["N1"].at[0], sem["rt"].at[0])
 
@@ -364,9 +356,9 @@
 
     for i in range(1, nx):
         t = xed(i)
-        sl = pl.ds(pl.multiple_of(own * (2 * t + c), own), own)
+        sl = pl.ds(pl.multiple_of(chip * t, chip), chip)
         send(v["W2"].at[sl, :], v["RR"].at[x], sem["srr"], sem["rrr"], to_x(t))
-    sl = pl.ds(pl.multiple_of(own * cb, own), own)
+    sl = pl.ds(pl.multiple_of(chip * x, chip), chip)
     mine = pltpu.make_async_copy(v["W2"].at[sl, :], v["RR"].at[x], sem["ld"].at[5])
     mine.start()
     far_sums(v["S2"], v["Sc2"], v["X12"], v["X1c2"], v["T2"], v["Tc2"], v["XM2"], v["X22"], v["X2c2"], 1)
@@ -374,14 +366,12 @@
     put_one = pltpu.make_async_copy(v["NW"], new1, sem["ld"].at[6])
     put_one.start()
 
-    wait(v["C1"].at[pl.ds(0, nx)], sem["rct"].at[0])
-    near_one = nearest(v["C1"], v["R1"])
     mine.wait()
     wait(v["RR"].at[pl.ds(0, nx - 1)], sem["rrr"])
     for xx in range(nx):
         ta = xx + (xx + 1) // 2
         v["R2"][:, ta * LANES : (ta + 1) * LANES] = v["RR"][xx, :, 0:LANES]
-    left_own = iota((own, LANES), 1) < HALF
+    left_own = iota((chip, LANES), 1) < HALF
     for y in range(nx // 2):
         tb = 1 + 3 * y
         v["R2"][:, tb * LANES : (tb + 1) * LANES] = jnp.where(
@@ -389,23 +379,17 @@
             v["RR"][2 * y, :, LANES:].astype(F32),
             v["RR"][2 * y + 1, :, LANES:].astype(F32),
         ).astype(BF16)
-    wait(v["C2"].at[pl.ds(0, nx)], sem["rct"].at[1])
-    near_two = nearest(v["C2"], v["R2"])
+    wait(v["C2"].at[pl.ds(0, nx - 1)], sem["rc"].at[1])
+    mins_two, psq_two = nearest(v["C2"], v["R2"])
+    v["D0"][c, 1] = mins_two
+    send(v["D0"].at[c], v["D0"].at[c], sem["sd"].at[0], sem["rd"].at[0], sib)
+    wait(v["D0"].at[0], sem["rd"].at[0])
     lane = iota((1, LANES), 1)
-    v["D0"][c] = jnp.where(lane == 0, near_one, jnp.where(lane == 1, near_two, 0.0))
-    send(v["D0"].at[c], v["D0"].at[c], sem["sd"].at[0], sem["rd"].at[0], sib)
-
-    wait(v["D0"].at[0], sem["rd"].at[0])
-    v["D1"][x] = v["D0"][0] + v["D0"][1]
+    tot_one = jnp.sum(jnp.minimum(v["D0"][0, 0], v["D0"][1, 0]), axis=1, keepdims=True) + psq_one
+    tot_two = jnp.sum(jnp.minimum(v["D0"][0, 1], v["D0"][1, 1]), axis=1, keepdims=True) + psq_two
+    v["D1"][x] = jnp.where(lane == 0, tot_one, jnp.where(lane == 1, tot_two, 0.0))
     for i in range(1, nx):
         send(v["D1"].at[x], v["D1"].at[x], sem["sd"].at[1], sem["rd"].at[1], to_x(xed(i)))
-    wait(v["D1"].at[pl.ds(0, nx - 1)], sem["rd"].at[1])
-    tot = v["D1"][0]
-    for i in range(1, nx):
-        tot = tot + v["D1"][i]
-    v["D2"][cl, q] = tot
-    for o in range(1, nq):
-        send(v["D2"].at[cl, q], v["D2"].at[cl, q], sem["sd"].at[2], sem["rd"].at[2], to_z(zed(WIN * o)))
 
     new_lo, new_hi, new_b = finish(v["T2"], v["Tc2"], v["X22"], v["X2c2"], v["C2"], 1)
     v["NC"][0:g, :] = new_lo
@@ -423,6 +407,14 @@
         @pl.when(t == x)
         def _():
             pltpu.make_async_copy(src, v["Y"].at[x], sem["ly"]).start()
+
+    wait(v["D1"].at[pl.ds(0, nx - 1)], sem["rd"].at[1])
+    tot = v["D1"][0]
+    for i in range(1, nx):
+        tot = tot + v["D1"][i]
+    v["D2"][cl, q] = tot
+    for o in range(1, nq):
+        send(v["D2"].at[cl, q], v["D2"].at[cl, q], sem["sd"].at[2], sem["rd"].at[2], to_z(zed(WIN * o)))
 
     def pass_dist():
         wait(v["D2"].at[0, pl.ds(0, nq - 1)], sem["rd"].at[2])
@@ -469,7 +461,6 @@
         wait(v["X11"].at[0, pl.ds(0, nq - 1)], sem["s2"].at[k])
         wait(v["X2c1"], sem["s2c"].at[k])
         wait(v["C1"].at[pl.ds(0, nx - 1)], sem["sc"].at[k])
-        wait(v["C1"].at[pl.ds(0, nx)], sem["sct"].at[k])
     wait(v["N1"].at[0, 0, pl.ds(0, nq - 1)], sem["sf"].at[0])
     wait(v["N1"].at[0, pl.ds(0, 3)], sem["sl"].at[0])
     wait(v["OA1"].at[pl.ds(0, nx - 1)], sem["so"].at[0])
@@ -503,7 +494,7 @@
     def local(points, code_one, code_two, cent_one, cent_two):
         npts, width = points.shape
         rows = cent_one.shape[0]
-        own = npts // (2 * nx)
+        chip = npts // nx
         g = 2 * rows // nz
         ch = 3 * g
         vm = pltpu.VMEM
@@ -513,10 +504,10 @@
             "W2": vm((npts, 2 * LANES), BF16),
             "CT": vm((npts, LANES), F32),
             "L": vm((2 * nx * rows, 2 * LANES), BF16),
-            "R1": vm((own, width), BF16),
-            "R2": vm((own, width), BF16),
-            "RR": vm((nx, own, 2 * LANES), BF16),
-            "D0": vm((2, 1, LANES), F32),
+            "R1": vm((chip, width), BF16),
+            "R2": vm((chip, width), BF16),
+            "RR": vm((nx, chip, 2 * LANES), BF16),
+            "D0": vm((2, 2, 1, chip), F32),
             "D1": vm((nx, 1, LANES), F32),
             "D2": vm((WIN, nq, 1, LANES), F32),
         }
@@ -528,7 +519,7 @@
         v["Y"] = vm((nx, 2 * g, LANES), BF16)
         v["O"] = vm((2 * nq, g, width), BF16)
         for k in ("1", "2"):
-            v["C" + k] = vm((2 * nx, rows, width), BF16)
+            v["C" + k] = vm((nx, rows, width), BF16)
             v["S" + k] = vm((WIN, nq, ch, LANES), F32)
             v["Sc" + k] = vm((WIN, nq, 1, LANES), F32)
             v["X1" + k] = vm((3, nq, ch, LANES), F32)
@@ -547,12 +538,13 @@
             "st": dma((1,)), "rt": dma((1,)),
             "so": dma((2,)), "ro": dma((2,)), "lo": dma((2,)),
             "sy": dma(()), "ry": dma(()), "ly": dma(()),
-            "sc": dma((2,)), "rc": dma((2,)), "sct": dma((2,)), "rct": dma((2,)),
+            "sc": dma((2,)), "rc": dma((2,)),
             "srr": dma(()), "rrr": dma(()),
             "sd": dma((4,)), "rd": dma((4,)),
         }
         hbm = pl.BlockSpec(memory_space=pl.ANY)
         vmem = pl.BlockSpec(memory_space=pltpu.VMEM)
+        far = pl.BlockSpec(memory_space=pltpu.HBM)
         new_one, new_two, dist = pl.pallas_call(
             functools.partial(kernel, nz, nx),
             out_shape=(
@@ -560,11 +552,11 @@
                 jax.ShapeDtypeStruct((2 * nq, g, width), BF16),
                 jax.ShapeDtypeStruct((1, LANES), F32),
             ),
-            in_specs=[hbm, vmem, vmem, hbm, hbm],
+            in_specs=[far, vmem, vmem, far, far],
             out_specs=(hbm, hbm, vmem),
             scratch_shapes=[v, sem],
             compiler_params=pltpu.CompilerParams(
-                collective_id=0, has_side_effects=True, vmem_limit_bytes=60 * 1024 * 1024
+                collective_id=0, has_side_effects=True, vmem_limit_bytes=53 * 1024 * 1024
             ),
         )(points, code_one.reshape(1, npts), code_two.reshape(1, npts), cent_one, cent_two)
         return new_one, new_two.reshape(rows, width), dist[0, :2]

time: 162 us -> 160 us (0.988)
  Pallas kernels: 157 us -> 155 us
    pallas_call x1, Pallas kernels: 157 us -> 155 us  [local(): pl.pallas_call(functools.partial(kernel, nz, nx), out_shape=(jax.ShapeDty...]
    unnamed x2 -> x6, local copies, waits for them, and re-layouts: 3.53 us -> 2.88 us
where the time goes in v3:
time: 160 us; the launch traced here: 159 us
  Pallas kernels  155 us (97%)
  local copies, waits for them, and re-layouts  3.39 us (2%)
    pallas_call x1, Pallas kernels, local(): pl.pallas_call(functools.partial(kernel, nz, nx), out_shape=(jax.ShapeDty...  155 us

profile of v3, /device:TPU:38, one launch (start us, length us, event | category | flops | bytes accessed | tf_op | source)
XLA Modules:
  0.0 159.2 jit_solution(11496493228807209564)
XLA Ops:
  0.6 0.0 copy-start
  0.6 0.7 copy-done
  1.3 0.0 copy-start.1
  1.3 0.7 copy-done.1
  2.0 155.1 %shard_map.76 = (bf16[256,768]{1,0:T(8,128)(2,1)S(1)}, bf16[16,16,768]{2,1,0:T(8,128)(2,1)S(1)}, f32[1,128]{1,0:T(1,128)S(1)}) custom-call(bf16[2048,768]{1,0:T(8,128)(2,1)} %pts.1, s32[1,2048]{1,0:T(1,128)S(1)} %bitcast.6, s32[1,2048]{1,0:T(1,128)S(1)} %bitcast.7, bf16[256,768]{1,0:T(8,128)(2,1)} %cent1.1, bf16[256,768]{1,0:T(8,128)(2,1)} %cent2.1), custom_call_target="tpu_custom_call" | custom-call | tf_op jit(solution)/shard_map/pallas_call | solution.py:548
  157.2 0.5 slice_bitcast_fusion
  157.7 0.7 copy.10
  158.4 0.7 copy.11
Async XLA Ops:
  0.6 0.7 copy-start
  1.3 0.7 copy-start.1

commit v4 on v3

--- a/solution.py
+++ b/solution.py
@@ -193,23 +193,18 @@
         ct = lax.rem(t, WIN)
         return 2 * lax.rem(ct, 2) + ct // 2
 
-    def tree(at, k, near_sends):
+    def far_gather(at, k, near_sends):
         slots = (1, -1, 2, -2, 3, -3, 4)
 
         def far_send(ref, d, to):
             send(ref, ref, sem["sf"].at[k], sem["rf"].at[k, slots.index(d)], to_z(zq(to)))
 
-        for d in (2, -2, 1, -1):
+        for d in slots[::-1]:
             far_send(at(q), d, d)
         near_sends(q)
         for d in slots:
             qs = qm(-d)
             wait(at(qs), sem["rf"].at[k, slots.index(d)])
-            if d == 2:
-                far_send(at(qs), 4, 2)
-                far_send(at(qs), 3, 1)
-            if d == -2:
-                far_send(at(qs), -3, -1)
             near_sends(qs)
 
     def gather(N):
@@ -219,7 +214,7 @@
             for i in range(3):
                 send(N.at[c, ci, qs], N.at[c, ci, qs], sem["sl"].at[0], sem["rl"].at[0, i], to_z(zed(s * NEAR[i])))
 
-        tree(lambda qs: N.at[c, ci, qs], 0, near_sends)
+        far_gather(lambda qs: N.at[c, ci, qs], 0, near_sends)
         send(N.at[c, ci], N.at[c, ci], sem["st"].at[0], sem["rt"].at[0], sib)
         for i in (2, 1, 0):
             cs = cidx(zed(-s * NEAR[i]))
@@ -232,7 +227,7 @@
             for i, step in enumerate((1, -1, 2 * s)):
                 send(at, at, sem["sl"].at[1], sem["rl"].at[1, i], to_z(zed(step)))
 
-        tree(lambda qs: O.at[2 * qs + e], 1, near_sends)
+        far_gather(lambda qs: O.at[2 * qs + e], 1, near_sends)
 
     def out_parts(N, t):
         pair = pl.ds(2 * (t // 2), 2)

time: 160 us -> 160 us (level)
  no operation moved by 1% of the time
where the time goes in v4:
time: 160 us; the launch traced here: 159 us
  Pallas kernels  155 us (97%)
  local copies, waits for them, and re-layouts  3.39 us (2%)
    pallas_call x1, Pallas kernels, local(): pl.pallas_call(functools.partial(kernel, nz, nx), out_shape=(jax.ShapeDty...  155 us

profile of v4, /device:TPU:38, one launch (start us, length us, event | category | flops | bytes accessed | tf_op | source)
XLA Modules:
  0.0 158.6 jit_solution(4713222182970280337)
XLA Ops:
  0.6 0.0 copy-start
  0.6 0.7 copy-done
  1.3 0.0 copy-start.1
  1.3 0.7 copy-done.1
  2.0 154.6 %shard_map.76 = (bf16[256,768]{1,0:T(8,128)(2,1)S(1)}, bf16[16,16,768]{2,1,0:T(8,128)(2,1)S(1)}, f32[1,128]{1,0:T(1,128)S(1)}) custom-call(bf16[2048,768]{1,0:T(8,128)(2,1)} %pts.1, s32[1,2048]{1,0:T(1,128)S(1)} %bitcast.6, s32[1,2048]{1,0:T(1,128)S(1)} %bitcast.7, bf16[256,768]{1,0:T(8,128)(2,1)} %cent1.1, bf16[256,768]{1,0:T(8,128)(2,1)} %cent2.1), custom_call_target="tpu_custom_call" | custom-call | tf_op jit(solution)/shard_map/pallas_call | solution.py:543
  156.6 0.5 slice_bitcast_fusion
  157.1 0.7 copy.10
  157.9 0.7 copy.11
Async XLA Ops:
  0.6 0.7 copy-start
  1.3 0.7 copy-start.1

commit v5 on v4

--- a/solution.py
+++ b/solution.py
@@ -16,7 +16,7 @@
 NEAR = (-2, -1, 1)
 
 
-TREE = (4, 3, -3, 1, -1, 2, -2)
+TREE = (4, 3, -3, 2, -2, 1, -1)
 
 
 def iota(shape, dim):
@@ -71,8 +71,6 @@
     barrier = pltpu.get_barrier_semaphore()
     for step in (-2, -1, 1, 2):
         pl.semaphore_signal(barrier, inc=1, device_id=to_z(zed(step)), device_id_type=MESH)
-    for o in range(1, nq):
-        pl.semaphore_signal(barrier, inc=1, device_id=to_z(zed(WIN * o)), device_id_type=MESH)
     for i in range(1, nx):
         pl.semaphore_signal(barrier, inc=1, device_id=to_x(xed(i)), device_id_type=MESH)
     pl.semaphore_signal(barrier, inc=1, device_id=sib, device_id_type=MESH)
@@ -138,39 +136,33 @@
             qd = lax.rem(qt + d * s + 2 * nq, nq)
             send(S.at[ct, qd], X1.at[i, qd], sem["s1"].at[k], sem["r1"].at[k, qd], to_z(t))
 
-    def far_sums(S, Sc, X1, X1c, T, Tc, XM, X2, X2c, k):
+    def far_sums(S, Sc, X1, X1c, T, Tc, XM, XMc, X2, X2c, k):
+        wait(X1c, sem["r1c"].at[k])
         for d in TREE + (0,):
             qd = qm(d)
             wait(X1.at[:, 0], sem["r1"].at[k, qd])
             t = S[cl, qd] + X1[0, qd] + X1[1, qd] + X1[2, qd]
-            if d == 2:
-                wait(XM.at[0], sem["rm"].at[k, 0])
-                wait(XM.at[1], sem["rm"].at[k, 1])
-                t = t + XM[0] + XM[1]
-            if d == -2:
-                wait(XM.at[2], sem["rm"].at[k, 2])
-                t = t + XM[2]
+            n = Sc[cl, qd] + X1c[0, qd] + X1c[1, qd] + X1c[2, qd]
+            for m in {2: (0, 1), -2: (2,)}.get(d, ()):
+                wait(XM.at[m], sem["rm"].at[k, m])
+                wait(XMc.at[m], sem["rmc"].at[k, m])
+                t = t + XM[m]
+                n = n + XMc[m]
             T[qd] = t
-            if d == 4:
-                send(T.at[qd], XM.at[0], sem["s2"].at[k], sem["rm"].at[k, 0], to_z(zq(2)))
-                wait(X1c, sem["r1c"].at[k])
-                Tc[...] = Sc[cl] + X1c[0] + X1c[1] + X1c[2]
-                for o in range(1, nq):
-                    qo = lax.rem(q + o, nq)
-                    send(Tc.at[qo], X2c.at[o - 1], sem["s2c"].at[k], sem["r2c"].at[k], to_z(zed(WIN * o)))
-            elif d == 3:
-                send(T.at[qd], XM.at[1], sem["s2"].at[k], sem["rm"].at[k, 1], to_z(zq(1)))
-            elif d == -3:
-                send(T.at[qd], XM.at[2], sem["s2"].at[k], sem["rm"].at[k, 2], to_z(zq(-1)))
+            Tc[qd] = n
+            if d in (4, 3, -3):
+                m = (4, 3, -3).index(d)
+                to = to_z(zq((2, 1, -1)[m]))
+                send(T.at[qd], XM.at[m], sem["s2"].at[k], sem["rm"].at[k, m], to)
+                send(Tc.at[qd], XMc.at[m], sem["s2c"].at[k], sem["rmc"].at[k, m], to)
             elif d != 0:
-                at = (1, -1, 2, -2).index(d)
-                send(T.at[qd], X2.at[at], sem["s2"].at[k], sem["r2"].at[k], to_z(zq(d)))
+                m = (1, -1, 2, -2).index(d)
+                send(T.at[qd], X2.at[m], sem["s2"].at[k], sem["r2"].at[k], to_z(zq(d)))
+                send(Tc.at[qd], X2c.at[m], sem["s2c"].at[k], sem["r2c"].at[k], to_z(zq(d)))
 
     def finish(T, Tc, X2, X2c, C, k):
         wait(X2c, sem["r2c"].at[k])
-        cnt = Tc[q]
-        for o in range(nq - 1):
-            cnt = cnt + X2c[o]
+        cnt = Tc[q] + X2c[0] + X2c[1] + X2c[2] + X2c[3]
         wait(X2, sem["r2"].at[k])
         tot = T[q] + X2[0] + X2[1] + X2[2] + X2[3]
         full = jnp.broadcast_to(cnt, (g, LANES))
@@ -199,12 +191,14 @@
         def far_send(ref, d, to):
             send(ref, ref, sem["sf"].at[k], sem["rf"].at[k, slots.index(d)], to_z(zq(to)))
 
-        for d in slots[::-1]:
+        for d in slots[5::-1]:
             far_send(at(q), d, d)
         near_sends(q)
         for d in slots:
             qs = qm(-d)
             wait(at(qs), sem["rf"].at[k, slots.index(d)])
+            if d == 2:
+                far_send(at(qs), 4, 2)
             near_sends(qs)
 
     def gather(N):
@@ -286,19 +280,36 @@
     loads[2].wait()
     loads[3].wait()
     loads[4].wait()
-    pl.semaphore_wait(barrier, 4 + (nq - 1) + (nx - 1) + 1)
+    pl.semaphore_wait(barrier, 4 + (nx - 1) + 1)
+
+    def tell(k, step):
+        pl.semaphore_signal(sem["lv"].at[k, 0], inc=1, device_id=to_z(zed(-step)), device_id_type=MESH)
+        pl.semaphore_signal(sem["lv"].at[k, 1], inc=1, device_id=to_z(zed(step)), device_id_type=MESH)
+
+    def told(k):
+        pl.semaphore_wait(sem["lv"].at[k, 0], 1)
+        pl.semaphore_wait(sem["lv"].at[k, 1], 1)
+
+    tell(0, 2)
 
     for i in range(3):
         class_sends(i, v["S1"], v["Sc1"], v["X11"], v["X1c1"], 0)
-    for k, C in enumerate((v["C1"], v["C2"])):
+    def cent_sends(C, k):
         for i in range(1, nx):
             send(C.at[x], C.at[x], sem["sc"].at[k], sem["rc"].at[k], to_x(xed(i)))
+
+    cent_sends(v["C1"], 0)
 
     for b in range(npts // LANES):
         row = code1[0:1, b * LANES : (b + 1) * LANES].astype(F32)
         v["CT"][b * LANES : (b + 1) * LANES, :] = jnp.transpose(jnp.broadcast_to(row, (LANES, LANES)))
 
-    far_sums(v["S1"], v["Sc1"], v["X11"], v["X1c1"], v["T1"], v["Tc1"], v["XM1"], v["X21"], v["X2c1"], 0)
+    told(0)
+    tell(1, WIN)
+    told(1)
+    tell(2, 2 * WIN)
+    far_sums(v["S1"], v["Sc1"], v["X11"], v["X1c1"], v["T1"], v["Tc1"], v["XM1"], v["XMc1"], v["X21"], v["X2c1"], 0)
+    cent_sends(v["C2"], 1)
     wait(v["C1"].at[pl.ds(0, nx - 1)], sem["rc"].at[0])
     mins_one, psq_one = nearest(v["C1"], v["R1"])
     v["D0"][c, 0] = mins_one
@@ -306,8 +317,8 @@
     v["N1"][c, 2 * par + e, q, 0:g, :] = new_lo
     v["N1"][c, 2 * par + e, q, g : 2 * g, :] = new_hi
     v["N1"][c, 2 * par + e, q, 2 * g :, :] = new_b
+    told(2)
     gather(v["N1"])
-    out_sends(v["N1"], v["OA1"], v["OB1"])
     wait(v["N1"].at[0], sem["rt"].at[0])
 
     kb = nq * g
@@ -356,10 +367,8 @@
     sl = pl.ds(pl.multiple_of(chip * x, chip), chip)
     mine = pltpu.make_async_copy(v["W2"].at[sl, :], v["RR"].at[x], sem["ld"].at[5])
     mine.start()
-    far_sums(v["S2"], v["Sc2"], v["X12"], v["X1c2"], v["T2"], v["Tc2"], v["XM2"], v["X22"], v["X2c2"], 1)
-    out_rows(v["OA1"], v["OB1"], v["NW"])
-    put_one = pltpu.make_async_copy(v["NW"], new1, sem["ld"].at[6])
-    put_one.start()
+    far_sums(v["S2"], v["Sc2"], v["X12"], v["X1c2"], v["T2"], v["Tc2"], v["XM2"], v["XMc2"], v["X22"], v["X2c2"], 1)
+    out_sends(v["N1"], v["OA1"], v["OB1"])
 
     mine.wait()
     wait(v["RR"].at[pl.ds(0, nx - 1)], sem["rrr"])
@@ -411,6 +420,10 @@
     for o in range(1, nq):
         send(v["D2"].at[cl, q], v["D2"].at[cl, q], sem["sd"].at[2], sem["rd"].at[2], to_z(zed(WIN * o)))
 
+    out_rows(v["OA1"], v["OB1"], v["NW"])
+    put_one = pltpu.make_async_copy(v["NW"], new1, sem["ld"].at[6])
+    put_one.start()
+
     def pass_dist():
         wait(v["D2"].at[0, pl.ds(0, nq - 1)], sem["rd"].at[2])
         for i in range(3):
@@ -454,7 +467,7 @@
         wait(v["X11"], sem["s1"].at[k])
         wait(v["X1c1"], sem["s1c"].at[k])
         wait(v["X11"].at[0, pl.ds(0, nq - 1)], sem["s2"].at[k])
-        wait(v["X2c1"], sem["s2c"].at[k])
+        wait(v["X1c1"].at[0, pl.ds(0, nq - 1)], sem["s2c"].at[k])
         wait(v["C1"].at[pl.ds(0, nx - 1)], sem["sc"].at[k])
     wait(v["N1"].at[0, 0, pl.ds(0, nq - 1)], sem["sf"].at[0])
     wait(v["N1"].at[0, pl.ds(0, 3)], sem["sl"].at[0])
@@ -523,12 +536,13 @@
             v["Tc" + k] = vm((nq, 1, LANES), F32)
             v["XM" + k] = vm((3, ch, LANES), F32)
             v["X2" + k] = vm((4, ch, LANES), F32)
-            v["X2c" + k] = vm((nq - 1, 1, LANES), F32)
+            v["X2c" + k] = vm((4, 1, LANES), F32)
+            v["XMc" + k] = vm((3, 1, LANES), F32)
         dma = pltpu.SemaphoreType.DMA
         sem = {
             "ld": dma((8,)),
             "s1": dma((2,)), "r1": dma((2, nq)), "s1c": dma((2,)), "r1c": dma((2,)),
-            "rm": dma((2, 3)), "s2": dma((2,)), "r2": dma((2,)), "s2c": dma((2,)), "r2c": dma((2,)),
+            "rm": dma((2, 3)), "rmc": dma((2, 3)), "lv": pltpu.SemaphoreType.REGULAR((3, 2)), "s2": dma((2,)), "r2": dma((2,)), "s2c": dma((2,)), "r2c": dma((2,)),
             "sf": dma((2,)), "rf": dma((2, nq - 1)), "sl": dma((2,)), "rl": dma((2, 3)),
             "st": dma((1,)), "rt": dma((1,)),
             "so": dma((2,)), "ro": dma((2,)), "lo": dma((2,)),

time: 160 us -> 155 us (0.969)
  Pallas kernels: 155 us -> 148 us
    pallas_call x1, Pallas kernels: 155 us -> 148 us  [local(): pl.pallas_call(functools.partial(kernel, nz, nx), out_shape=(jax.ShapeDty...]
where the time goes in v5:
time: 155 us; the launch traced here: 153 us
  Pallas kernels  148 us (95%)
  local copies, waits for them, and re-layouts  3.39 us (2%)
    pallas_call x1, Pallas kernels, local(): pl.pallas_call(functools.partial(kernel, nz, nx), out_shape=(jax.ShapeDty...  148 us

profile of v5, /device:TPU:38, one launch (start us, length us, event | category | flops | bytes accessed | tf_op | source)
XLA Modules:
  0.0 152.5 jit_solution(6747234554621630652)
XLA Ops:
  0.6 0.0 copy-start
  0.6 0.7 copy-done
  1.3 0.0 copy-start.1
  1.3 0.7 copy-done.1
  2.0 148.5 %shard_map.76 = (bf16[256,768]{1,0:T(8,128)(2,1)S(1)}, bf16[16,16,768]{2,1,0:T(8,128)(2,1)S(1)}, f32[1,128]{1,0:T(1,128)S(1)}) custom-call(bf16[2048,768]{1,0:T(8,128)(2,1)} %pts.1, s32[1,2048]{1,0:T(1,128)S(1)} %bitcast.6, s32[1,2048]{1,0:T(1,128)S(1)} %bitcast.7, bf16[256,768]{1,0:T(8,128)(2,1)} %cent1.1, bf16[256,768]{1,0:T(8,128)(2,1)} %cent2.1), custom_call_target="tpu_custom_call" | custom-call | tf_op jit(solution)/shard_map/pallas_call | solution.py:557
  150.5 0.5 slice_bitcast_fusion
  151.0 0.7 copy.10
  151.8 0.7 copy.11
Async XLA Ops:
  0.6 0.7 copy-start
  1.3 0.7 copy-start.1

commit v6 on v5

--- a/solution.py
+++ b/solution.py
@@ -136,7 +136,7 @@
             qd = lax.rem(qt + d * s + 2 * nq, nq)
             send(S.at[ct, qd], X1.at[i, qd], sem["s1"].at[k], sem["r1"].at[k, qd], to_z(t))
 
-    def far_sums(S, Sc, X1, X1c, T, Tc, XM, XMc, X2, X2c, k):
+    def far_sums(S, Sc, X1, X1c, T, Tc, XM, XMc, X2, X2c, k, beside):
         wait(X1c, sem["r1c"].at[k])
         for d in TREE + (0,):
             qd = qm(d)
@@ -155,6 +155,8 @@
                 to = to_z(zq((2, 1, -1)[m]))
                 send(T.at[qd], XM.at[m], sem["s2"].at[k], sem["rm"].at[k, m], to)
                 send(Tc.at[qd], XMc.at[m], sem["s2c"].at[k], sem["rmc"].at[k, m], to)
+                if d == -3:
+                    beside()
             elif d != 0:
                 m = (1, -1, 2, -2).index(d)
                 send(T.at[qd], X2.at[m], sem["s2"].at[k], sem["r2"].at[k], to_z(zq(d)))
@@ -294,11 +296,17 @@
 
     for i in range(3):
         class_sends(i, v["S1"], v["Sc1"], v["X11"], v["X1c1"], 0)
-    def cent_sends(C, k):
-        for i in range(1, nx):
-            send(C.at[x], C.at[x], sem["sc"].at[k], sem["rc"].at[k], to_x(xed(i)))
-
-    cent_sends(v["C1"], 0)
+    right, left_x, over = xed(1), xed(nx - 1), xed(2)
+    half = (pl.ds(0, rows // 2), pl.ds(rows // 2, rows // 2))
+
+    def cent_pass(C, k):
+        for side, (src, to) in enumerate(((left_x, right), (right, left_x))):
+            wait(C.at[src], sem["rc"].at[k, side])
+            send(C.at[src, half[side]], C.at[src, half[side]], sem["scf"].at[k], sem["rcf"].at[k], to_x(to))
+
+    for k, C in enumerate((v["C1"], v["C2"])):
+        send(C.at[x], C.at[x], sem["sc"].at[k], sem["rc"].at[k, 0], to_x(right))
+        send(C.at[x], C.at[x], sem["sc"].at[k], sem["rc"].at[k, 1], to_x(left_x))
 
     for b in range(npts // LANES):
         row = code1[0:1, b * LANES : (b + 1) * LANES].astype(F32)
@@ -308,9 +316,9 @@
     tell(1, WIN)
     told(1)
     tell(2, 2 * WIN)
-    far_sums(v["S1"], v["Sc1"], v["X11"], v["X1c1"], v["T1"], v["Tc1"], v["XM1"], v["XMc1"], v["X21"], v["X2c1"], 0)
-    cent_sends(v["C2"], 1)
-    wait(v["C1"].at[pl.ds(0, nx - 1)], sem["rc"].at[0])
+    far_sums(v["S1"], v["Sc1"], v["X11"], v["X1c1"], v["T1"], v["Tc1"], v["XM1"], v["XMc1"], v["X21"], v["X2c1"], 0, lambda: cent_pass(v["C1"], 0))
+    cent_pass(v["C2"], 1)
+    wait(v["C1"].at[0], sem["rcf"].at[0])
     mins_one, psq_one = nearest(v["C1"], v["R1"])
     v["D0"][c, 0] = mins_one
     new_lo, new_hi, new_b = finish(v["T1"], v["Tc1"], v["X21"], v["X2c1"], v["C1"], 0)
@@ -360,18 +368,30 @@
         def _():
             class_sends(i, v["S2"], v["Sc2"], v["X12"], v["X1c2"], 1)
 
-    for i in range(1, nx):
-        t = xed(i)
-        sl = pl.ds(pl.multiple_of(chip * t, chip), chip)
-        send(v["W2"].at[sl, :], v["RR"].at[x], sem["srr"], sem["rrr"], to_x(t))
+    hc = chip // 2
+
+    def pts_of(t, part):
+        return pl.ds(pl.multiple_of(chip * t + hc * part, hc), hc)
+
+    for side, to in enumerate((right, left_x)):
+        send(v["W2"].at[pts_of(over, side), :], v["FW"].at[side], sem["sfw"], sem["rfw"].at[side], to_x(to))
+    for to in (right, left_x):
+        sl = pl.ds(pl.multiple_of(chip * to, chip), chip)
+        send(v["W2"].at[sl, :], v["RR"].at[x], sem["srr"], sem["rrr"], to_x(to))
+
+    def rows_pass():
+        for side, (src, to) in enumerate(((left_x, right), (right, left_x))):
+            wait(v["FW"].at[side], sem["rfw"].at[side])
+            send(v["FW"].at[side], v["RR"].at[src, pl.ds(hc * side, hc)], sem["sff"], sem["rrf"], to_x(to))
+
     sl = pl.ds(pl.multiple_of(chip * x, chip), chip)
     mine = pltpu.make_async_copy(v["W2"].at[sl, :], v["RR"].at[x], sem["ld"].at[5])
     mine.start()
-    far_sums(v["S2"], v["Sc2"], v["X12"], v["X1c2"], v["T2"], v["Tc2"], v["XM2"], v["XMc2"], v["X22"], v["X2c2"], 1)
-    out_sends(v["N1"], v["OA1"], v["OB1"])
+    far_sums(v["S2"], v["Sc2"], v["X12"], v["X1c2"], v["T2"], v["Tc2"], v["XM2"], v["XMc2"], v["X22"], v["X2c2"], 1, rows_pass)
 
     mine.wait()
-    wait(v["RR"].at[pl.ds(0, nx - 1)], sem["rrr"])
+    wait(v["RR"].at[pl.ds(0, 2)], sem["rrr"])
+    wait(v["RR"].at[0], sem["rrf"])
     for xx in range(nx):
         ta = xx + (xx + 1) // 2
         v["R2"][:, ta * LANES : (ta + 1) * LANES] = v["RR"][xx, :, 0:LANES]
@@ -383,7 +403,7 @@
             v["RR"][2 * y, :, LANES:].astype(F32),
             v["RR"][2 * y + 1, :, LANES:].astype(F32),
         ).astype(BF16)
-    wait(v["C2"].at[pl.ds(0, nx - 1)], sem["rc"].at[1])
+    wait(v["C2"].at[0], sem["rcf"].at[1])
     mins_two, psq_two = nearest(v["C2"], v["R2"])
     v["D0"][c, 1] = mins_two
     send(v["D0"].at[c], v["D0"].at[c], sem["sd"].at[0], sem["rd"].at[0], sib)
@@ -420,9 +440,7 @@
     for o in range(1, nq):
         send(v["D2"].at[cl, q], v["D2"].at[cl, q], sem["sd"].at[2], sem["rd"].at[2], to_z(zed(WIN * o)))
 
-    out_rows(v["OA1"], v["OB1"], v["NW"])
-    put_one = pltpu.make_async_copy(v["NW"], new1, sem["ld"].at[6])
-    put_one.start()
+    out_sends(v["N1"], v["OA1"], v["OB1"])
 
     def pass_dist():
         wait(v["D2"].at[0, pl.ds(0, nq - 1)], sem["rd"].at[2])
@@ -454,6 +472,9 @@
         wait(v["O"].at[pl.ds(0, nq)], sem["rl"].at[1, 0])
         wait(v["O"].at[pl.ds(0, nq)], sem["rl"].at[1, 1])
 
+    out_rows(v["OA1"], v["OB1"], v["NW"])
+    put_one = pltpu.make_async_copy(v["NW"], new1, sem["ld"].at[6])
+    put_one.start()
     put_two = pltpu.make_async_copy(v["O"], new2, sem["ld"].at[7])
     put_two.start()
 
@@ -468,13 +489,16 @@
         wait(v["X1c1"], sem["s1c"].at[k])
         wait(v["X11"].at[0, pl.ds(0, nq - 1)], sem["s2"].at[k])
         wait(v["X1c1"].at[0, pl.ds(0, nq - 1)], sem["s2c"].at[k])
-        wait(v["C1"].at[pl.ds(0, nx - 1)], sem["sc"].at[k])
+        wait(v["C1"].at[pl.ds(0, 2)], sem["sc"].at[k])
+        wait(v["C1"].at[0], sem["scf"].at[k])
     wait(v["N1"].at[0, 0, pl.ds(0, nq - 1)], sem["sf"].at[0])
     wait(v["N1"].at[0, pl.ds(0, 3)], sem["sl"].at[0])
     wait(v["OA1"].at[pl.ds(0, nx - 1)], sem["so"].at[0])
     wait(v["OB1"].at[pl.ds(0, nx - 1)], sem["so"].at[1])
     wait(v["N1"].at[0], sem["st"].at[0])
-    wait(v["RR"].at[pl.ds(0, nx - 1)], sem["srr"])
+    wait(v["RR"].at[pl.ds(0, 2)], sem["srr"])
+    wait(v["FW"], sem["sfw"])
+    wait(v["FW"], sem["sff"])
     wait(v["D0"].at[0], sem["sd"].at[0])
     wait(v["D1"].at[pl.ds(0, nx - 1)], sem["sd"].at[1])
     wait(v["D2"].at[0, pl.ds(0, nq - 1)], sem["sd"].at[2])
@@ -514,6 +538,7 @@
             "L": vm((2 * nx * rows, 2 * LANES), BF16),
             "R1": vm((chip, width), BF16),
             "R2": vm((chip, width), BF16),
+            "FW": vm((2, chip // 2, 2 * LANES), BF16),
             "RR": vm((nx, chip, 2 * LANES), BF16),
             "D0": vm((2, 2, 1, chip), F32),
             "D1": vm((nx, 1, LANES), F32),
@@ -547,7 +572,8 @@
             "st": dma((1,)), "rt": dma((1,)),
             "so": dma((2,)), "ro": dma((2,)), "lo": dma((2,)),
             "sy": dma(()), "ry": dma(()), "ly": dma(()),
-            "sc": dma((2,)), "rc": dma((2,)),
+            "sc": dma((2,)), "rc": dma((2, 2)), "scf": dma((2,)), "rcf": dma((2,)),
+            "sfw": dma(()), "rfw": dma((2,)), "sff": dma(()), "rrf": dma(()),
             "srr": dma(()), "rrr": dma(()),
             "sd": dma((4,)), "rd": dma((4,)),
         }

time: 155 us -> 157 us (1.013); the launches traced: 153 us -> 157 us
  Pallas kernels: 148 us -> 153 us
    pallas_call x1, Pallas kernels: 148 us -> 153 us  [local(): pl.pallas_call(functools.partial(kernel, nz, nx), out_shape=(jax.ShapeDty...]
where the time goes in v6:
time: 157 us
  Pallas kernels  153 us (97%)
  local copies, waits for them, and re-layouts  3.39 us (2%)
    pallas_call x1, Pallas kernels, local(): pl.pallas_call(functools.partial(kernel, nz, nx), out_shape=(jax.ShapeDty...  153 us

profile of v6, /device:TPU:38, one launch (start us, length us, event | category | flops | bytes accessed | tf_op | source)
XLA Modules:
  0.0 156.8 jit_solution(6601645838295135044)
XLA Ops:
  0.6 0.0 copy-start
  0.6 0.7 copy-done
  1.3 0.0 copy-start.1
  1.3 0.7 copy-done.1
  2.0 152.7 %shard_map.76 = (bf16[256,768]{1,0:T(8,128)(2,1)S(1)}, bf16[16,16,768]{2,1,0:T(8,128)(2,1)S(1)}, f32[1,128]{1,0:T(1,128)S(1)}) custom-call(bf16[2048,768]{1,0:T(8,128)(2,1)} %pts.1, s32[1,2048]{1,0:T(1,128)S(1)} %bitcast.6, s32[1,2048]{1,0:T(1,128)S(1)} %bitcast.7, bf16[256,768]{1,0:T(8,128)(2,1)} %cent1.1, bf16[256,768]{1,0:T(8,128)(2,1)} %cent2.1), custom_call_target="tpu_custom_call" | custom-call | tf_op jit(solution)/shard_map/pallas_call | solution.py:583
  154.8 0.5 slice_bitcast_fusion
  155.3 0.7 copy.10
  156.0 0.7 copy.11
Async XLA Ops:
  0.6 0.7 copy-start
  1.3 0.7 copy-start.1

commit v7 on v6

--- a/solution.py
+++ b/solution.py
@@ -317,7 +317,6 @@
     told(1)
     tell(2, 2 * WIN)
     far_sums(v["S1"], v["Sc1"], v["X11"], v["X1c1"], v["T1"], v["Tc1"], v["XM1"], v["XMc1"], v["X21"], v["X2c1"], 0, lambda: cent_pass(v["C1"], 0))
-    cent_pass(v["C2"], 1)
     wait(v["C1"].at[0], sem["rcf"].at[0])
     mins_one, psq_one = nearest(v["C1"], v["R1"])
     v["D0"][c, 0] = mins_one
@@ -327,38 +326,42 @@
     v["N1"][c, 2 * par + e, q, 2 * g :, :] = new_b
     told(2)
     gather(v["N1"])
-    wait(v["N1"].at[0], sem["rt"].at[0])
-
+    cent_pass(v["C2"], 1)
     kb = nq * g
-    for cc in range(2):
+    for part in range(2):
+        if part == 1:
+            wait(v["N1"].at[0], sem["rt"].at[0])
+        cc = c if part == 0 else 1 - c
         for k in range(WIN):
-            base = (cc * WIN + k) * 2 * kb
+            base = k * 2 * kb
             n = v["N1"][cc, k]
-            v["L"][base : base + kb, 0:LANES] = n[:, 0:g, :].reshape(kb, LANES)
-            v["L"][base + kb : base + 2 * kb, 0:LANES] = n[:, g : 2 * g, :].reshape(kb, LANES)
+            v["L"][part, base : base + kb, 0:LANES] = n[:, 0:g, :].reshape(kb, LANES)
+            v["L"][part, base + kb : base + 2 * kb, 0:LANES] = n[:, g : 2 * g, :].reshape(kb, LANES)
             b = n[:, 2 * g :, :].reshape(kb, LANES)
-            v["L"][base : base + kb, LANES : 2 * LANES] = b
-            v["L"][base + kb : base + 2 * kb, LANES : 2 * LANES] = pltpu.roll(b.astype(F32), HALF, 1).astype(BF16)
-
-    @pl.loop(0, npts // blk)
-    def _(i):
-        sl = pl.ds(pl.multiple_of(i * blk, blk), blk)
-        codes = v["CT"][sl, :]
-        parts = []
-        lane = iota((1, LANES), 1)
-        for j in range(2 * nx * rows // LANES):
-            r = lane + j * LANES
-            cc = r // (WIN * 2 * kb)
-            k = (r // (2 * kb)) & (WIN - 1)
-            hl = (r // kb) & 1
-            rq = (r // g) & (nq - 1)
-            lab = rows * (2 * (2 * (k // 2) + hl) + cc) + g * (2 * rq + (k & 1)) + (r & (g - 1))
-            parts.append(jnp.where(codes == lab.astype(F32), 1.0, 0.0).astype(BF16))
-        oh = jnp.concatenate(parts, axis=1)
-        looked = jnp.dot(oh, v["L"][...], preferred_element_type=F32)
-        res = v["P"][sl, :].astype(F32) - looked
-        v["W2"][sl, 0:LANES] = res[:, 0:LANES].astype(BF16)
-        v["W2"][sl, LANES : 2 * LANES] = jnp.where(hm_b, res[:, LANES:], 1.0).astype(BF16)
+            v["L"][part, base : base + kb, LANES : 2 * LANES] = b
+            v["L"][part, base + kb : base + 2 * kb, LANES : 2 * LANES] = pltpu.roll(b.astype(F32), HALF, 1).astype(BF16)
+
+        @pl.loop(0, npts // blk)
+        def _(i):
+            sl = pl.ds(pl.multiple_of(i * blk, blk), blk)
+            codes = v["CT"][sl, :]
+            parts = []
+            lane = iota((1, LANES), 1)
+            for j in range(nx * rows // LANES):
+                r = lane + j * LANES
+                k = r // (2 * kb)
+                hl = (r // kb) & 1
+                rq = (r // g) & (nq - 1)
+                lab = rows * (2 * (2 * (k // 2) + hl) + cc) + g * (2 * rq + (k & 1)) + (r & (g - 1))
+                parts.append(jnp.where(codes == lab.astype(F32), 1.0, 0.0).astype(BF16))
+            oh = jnp.concatenate(parts, axis=1)
+            looked = jnp.dot(oh, v["L"][part], preferred_element_type=F32)
+            if part == 0:
+                v["ACC"][sl, :] = looked
+            else:
+                res = v["P"][sl, :].astype(F32) - (v["ACC"][sl, :] + looked)
+                v["W2"][sl, 0:LANES] = res[:, 0:LANES].astype(BF16)
+                v["W2"][sl, LANES : 2 * LANES] = jnp.where(hm_b, res[:, LANES:], 1.0).astype(BF16)
 
     @pl.loop(0, WIN)
     def _(i):
@@ -388,6 +391,7 @@
     mine = pltpu.make_async_copy(v["W2"].at[sl, :], v["RR"].at[x], sem["ld"].at[5])
     mine.start()
     far_sums(v["S2"], v["Sc2"], v["X12"], v["X1c2"], v["T2"], v["Tc2"], v["XM2"], v["XMc2"], v["X22"], v["X2c2"], 1, rows_pass)
+    out_sends(v["N1"], v["OA1"], v["OB1"])
 
     mine.wait()
     wait(v["RR"].at[pl.ds(0, 2)], sem["rrr"])
@@ -440,7 +444,9 @@
     for o in range(1, nq):
         send(v["D2"].at[cl, q], v["D2"].at[cl, q], sem["sd"].at[2], sem["rd"].at[2], to_z(zed(WIN * o)))
 
-    out_sends(v["N1"], v["OA1"], v["OB1"])
+    out_rows(v["OA1"], v["OB1"], v["NW"])
+    put_one = pltpu.make_async_copy(v["NW"], new1, sem["ld"].at[6])
+    put_one.start()
 
     def pass_dist():
         wait(v["D2"].at[0, pl.ds(0, nq - 1)], sem["rd"].at[2])
@@ -472,9 +478,6 @@
         wait(v["O"].at[pl.ds(0, nq)], sem["rl"].at[1, 0])
         wait(v["O"].at[pl.ds(0, nq)], sem["rl"].at[1, 1])
 
-    out_rows(v["OA1"], v["OB1"], v["NW"])
-    put_one = pltpu.make_async_copy(v["NW"], new1, sem["ld"].at[6])
-    put_one.start()
     put_two = pltpu.make_async_copy(v["O"], new2, sem["ld"].at[7])
     put_two.start()
 
@@ -535,7 +538,8 @@
             "W": vm((npts, 2 * LANES), BF16),
             "W2": vm((npts, 2 * LANES), BF16),
             "CT": vm((npts, LANES), F32),
-            "L": vm((2 * nx * rows, 2 * LANES), BF16),
+            "L": vm((2, nx * rows, 2 * LANES), BF16),
+            "ACC": vm((npts, 2 * LANES), F32),
             "R1": vm((chip, width), BF16),
             "R2": vm((chip, width), BF16),
             "FW": vm((2, chip // 2, 2 * LANES), BF16),

time: 157 us -> 158 us (level)
  no operation moved by 1% of the time
where the time goes in v7:
time: 158 us
  Pallas kernels  154 us (97%)
  local copies, waits for them, and re-layouts  3.39 us (2%)
    pallas_call x1, Pallas kernels, local(): pl.pallas_call(functools.partial(kernel, nz, nx), out_shape=(jax.ShapeDty...  154 us

profile of v7, /device:TPU:38, one launch (start us, length us, event | category | flops | bytes accessed | tf_op | source)
XLA Modules:
  0.0 157.7 jit_solution(13514405048294214917)
XLA Ops:
  0.6 0.0 copy-start
  0.6 0.7 copy-done
  1.3 0.0 copy-start.1
  1.3 0.7 copy-done.1
  2.0 153.6 %shard_map.76 = (bf16[256,768]{1,0:T(8,128)(2,1)S(1)}, bf16[16,16,768]{2,1,0:T(8,128)(2,1)S(1)}, f32[1,128]{1,0:T(1,128)S(1)}) custom-call(bf16[2048,768]{1,0:T(8,128)(2,1)} %pts.1, s32[1,2048]{1,0:T(1,128)S(1)} %bitcast.6, s32[1,2048]{1,0:T(1,128)S(1)} %bitcast.7, bf16[256,768]{1,0:T(8,128)(2,1)} %cent1.1, bf16[256,768]{1,0:T(8,128)(2,1)} %cent2.1), custom_call_target="tpu_custom_call" | custom-call | tf_op jit(solution)/shard_map/pallas_call | solution.py:587
  155.7 0.5 slice_bitcast_fusion
  156.2 0.7 copy.10
  156.9 0.7 copy.11
Async XLA Ops:
  0.6 0.7 copy-start
  1.3 0.7 copy-start.1

commit v8 on v5

--- a/solution.py
+++ b/solution.py
@@ -298,6 +298,20 @@
         for i in range(1, nx):
             send(C.at[x], C.at[x], sem["sc"].at[k], sem["rc"].at[k], to_x(xed(i)))
 
+    right, left_x = xed(1), xed(nx - 1)
+    half = (pl.ds(0, rows // 2), pl.ds(rows // 2, rows // 2))
+
+    def cent_near():
+        C = v["C2"]
+        send(C.at[x], C.at[x], sem["sc"].at[1], sem["rcn"].at[0], to_x(right))
+        send(C.at[x], C.at[x], sem["sc"].at[1], sem["rcn"].at[1], to_x(left_x))
+
+    def cent_pass():
+        C = v["C2"]
+        for side, (src, to) in enumerate(((left_x, right), (right, left_x))):
+            wait(C.at[src], sem["rcn"].at[side])
+            send(C.at[src, half[side]], C.at[src, half[side]], sem["scf"], sem["rc"].at[1], to_x(to))
+
     cent_sends(v["C1"], 0)
 
     for b in range(npts // LANES):
@@ -309,7 +323,6 @@
     told(1)
     tell(2, 2 * WIN)
     far_sums(v["S1"], v["Sc1"], v["X11"], v["X1c1"], v["T1"], v["Tc1"], v["XM1"], v["XMc1"], v["X21"], v["X2c1"], 0)
-    cent_sends(v["C2"], 1)
     wait(v["C1"].at[pl.ds(0, nx - 1)], sem["rc"].at[0])
     mins_one, psq_one = nearest(v["C1"], v["R1"])
     v["D0"][c, 0] = mins_one
@@ -319,6 +332,7 @@
     v["N1"][c, 2 * par + e, q, 2 * g :, :] = new_b
     told(2)
     gather(v["N1"])
+    cent_near()
     wait(v["N1"].at[0], sem["rt"].at[0])
 
     kb = nq * g
@@ -368,6 +382,7 @@
     mine = pltpu.make_async_copy(v["W2"].at[sl, :], v["RR"].at[x], sem["ld"].at[5])
     mine.start()
     far_sums(v["S2"], v["Sc2"], v["X12"], v["X1c2"], v["T2"], v["Tc2"], v["XM2"], v["XMc2"], v["X22"], v["X2c2"], 1)
+    cent_pass()
     out_sends(v["N1"], v["OA1"], v["OB1"])
 
     mine.wait()
@@ -383,7 +398,7 @@
             v["RR"][2 * y, :, LANES:].astype(F32),
             v["RR"][2 * y + 1, :, LANES:].astype(F32),
         ).astype(BF16)
-    wait(v["C2"].at[pl.ds(0, nx - 1)], sem["rc"].at[1])
+    wait(v["C2"].at[0], sem["rc"].at[1])
     mins_two, psq_two = nearest(v["C2"], v["R2"])
     v["D0"][c, 1] = mins_two
     send(v["D0"].at[c], v["D0"].at[c], sem["sd"].at[0], sem["rd"].at[0], sib)
@@ -468,7 +483,7 @@
         wait(v["X1c1"], sem["s1c"].at[k])
         wait(v["X11"].at[0, pl.ds(0, nq - 1)], sem["s2"].at[k])
         wait(v["X1c1"].at[0, pl.ds(0, nq - 1)], sem["s2c"].at[k])
-        wait(v["C1"].at[pl.ds(0, nx - 1)], sem["sc"].at[k])
+        wait(v["C1"].at[pl.ds(0, nx - 1 - k)], sem["sc"].at[k])
     wait(v["N1"].at[0, 0, pl.ds(0, nq - 1)], sem["sf"].at[0])
     wait(v["N1"].at[0, pl.ds(0, 3)], sem["sl"].at[0])
     wait(v["OA1"].at[pl.ds(0, nx - 1)], sem["so"].at[0])
@@ -490,6 +505,7 @@
     def _():
         wait(v["Y"].at[pl.ds(0, 2)], sem["sy"])
 
+    wait(v["C1"].at[0], sem["scf"])
     put_one.wait()
     put_two.wait()
 
@@ -547,7 +563,7 @@
             "st": dma((1,)), "rt": dma((1,)),
             "so": dma((2,)), "ro": dma((2,)), "lo": dma((2,)),
             "sy": dma(()), "ry": dma(()), "ly": dma(()),
-            "sc": dma((2,)), "rc": dma((2,)),
+            "sc": dma((2,)), "rcn": dma((2,)), "scf": dma(()), "rc": dma((2,)),
             "srr": dma(()), "rrr": dma(()),
             "sd": dma((4,)), "rd": dma((4,)),
         }

time: 155 us -> 157 us (1.013)
  Pallas kernels: 148 us -> 151 us
    pallas_call x1, Pallas kernels: 148 us -> 151 us  [local(): pl.pallas_call(functools.partial(kernel, nz, nx), out_shape=(jax.ShapeDty...]
where the time goes in v8:
time: 157 us; the launch traced here: 155 us
  Pallas kernels  151 us (96%)
  local copies, waits for them, and re-layouts  3.39 us (2%)
    pallas_call x1, Pallas kernels, local(): pl.pallas_call(functools.partial(kernel, nz, nx), out_shape=(jax.ShapeDty...  151 us

profile of v8, /device:TPU:38, one launch (start us, length us, event | category | flops | bytes accessed | tf_op | source)
XLA Modules:
  0.0 154.9 jit_solution(10696692991295037152)
XLA Ops:
  0.6 0.0 copy-start
  0.6 0.7 copy-done
  1.3 0.0 copy-start.1
  1.3 0.7 copy-done.1
  2.0 150.8 %shard_map.76 = (bf16[256,768]{1,0:T(8,128)(2,1)S(1)}, bf16[16,16,768]{2,1,0:T(8,128)(2,1)S(1)}, f32[1,128]{1,0:T(1,128)S(1)}) custom-call(bf16[2048,768]{1,0:T(8,128)(2,1)} %pts.1, s32[1,2048]{1,0:T(1,128)S(1)} %bitcast.6, s32[1,2048]{1,0:T(1,128)S(1)} %bitcast.7, bf16[256,768]{1,0:T(8,128)(2,1)} %cent1.1, bf16[256,768]{1,0:T(8,128)(2,1)} %cent2.1), custom_call_target="tpu_custom_call" | custom-call | tf_op jit(solution)/shard_map/pallas_call | solution.py:573
  152.9 0.5 slice_bitcast_fusion
  153.4 0.7 copy.10
  154.1 0.7 copy.11
Async XLA Ops:
  0.6 0.7 copy-start
  1.3 0.7 copy-start.1
